TPU v7x, 32 devices: a 4x4x1 block of a 4x4x8 slice. The times are simulated.
32 devices in a mesh: mem: 1 (over z), row: 4 (over y), col: 4 (over x), core: 2 (over core).
Axes of the slice: x: 4, y: 4, z: 1, core: 2. Of those that a mesh axis runs over, the one named last changes fastest.
The devices are a block of a 4x4x8 slice.
Arguments:
- u_init: float32 [2048, 2048], P(('mem', 'row'), ('col', 'core'))
- forcing: float32 [2048, 2048], P(('mem', 'row'), ('col', 'core'))
- loss_weight: float32 [2048, 2048], P(('mem', 'row'), ('col', 'core'))
- stencil: float32 [3, 3], replicated
- gains: float32 [32], replicated
Outputs:
- output 1: float32 [2048, 2048], P(('mem', 'row'), ('col', 'core'))
- output 2: float32 [2048, 2048], P(('mem', 'row'), ('col', 'core'))
- output 3: float32 [2048, 2048], P(('mem', 'row'), ('col', 'core'))
All inputs are finite; a program needn't handle non-finite values.
Results may differ from a plain program's by a relative error of at most 0.001.
Values sent between devices are 32-bit elements.
A program may use at most 768 MiB of HBM per device.

v0:
```python
import jax
import jax.numpy as jnp
from jax import lax
from jax.sharding import PartitionSpec as P

DT = 0.01


def seg_len(num_steps):
    best_len = 1
    for cand_len in range(1, num_steps + 1):
        if num_steps % cand_len == 0 and cand_len * cand_len <= num_steps:
            best_len = cand_len
    return best_len


def stencil_apply(padded, weights):
    out_rows = padded.shape[0] - 2
    out_cols = padded.shape[1] - 2
    total_sum = None
    for row_off in range(3):
        for col_off in range(3):
            term_val = weights[row_off, col_off] * padded[row_off:row_off + out_rows, col_off:col_off + out_cols]
            total_sum = term_val if total_sum is None else total_sum + term_val
    return total_sum


def solution(mesh):
    row_size = mesh.shape["row"]
    col_size = mesh.shape["col"] * mesh.shape["core"]
    col_axes = ("col", "core")
    to_next_row = [(src_idx, (src_idx + 1) % row_size) for src_idx in range(row_size)]
    to_prev_row = [(src_idx, (src_idx - 1) % row_size) for src_idx in range(row_size)]
    to_next_col = [(src_idx, (src_idx + 1) % col_size) for src_idx in range(col_size)]
    to_prev_col = [(src_idx, (src_idx - 1) % col_size) for src_idx in range(col_size)]
    field_spec = P(("mem", "row"), ("col", "core"))

    def exchange(tile_vals, halo_depth):
        from_above = lax.ppermute(tile_vals[-halo_depth:], "row", to_next_row)
        from_below = lax.ppermute(tile_vals[:halo_depth], "row", to_prev_row)
        tall_tile = jnp.concatenate([from_above, tile_vals, from_below], axis=0)
        from_left = lax.ppermute(tall_tile[:, -halo_depth:], col_axes, to_next_col)
        from_right = lax.ppermute(tall_tile[:, :halo_depth], col_axes, to_prev_col)
        return jnp.concatenate([from_left, tall_tile, from_right], axis=1)

    def local_run(u_init, forcing, loss_weight, weights, gains):
        num_steps = gains.shape[0]
        seg_steps = seg_len(num_steps)
        gain_rows = gains.reshape(num_steps // seg_steps, seg_steps)
        flipped = weights[::-1, ::-1]

        def fwd_step(field_state, gain_val):
            padded = exchange(field_state, 1)
            return stencil_apply(padded, weights) + DT * (field_state - field_state * field_state * field_state) + gain_val * forcing

        def fwd_segment(field_state, gain_row):
            def step_body(inner_state, gain_val):
                return fwd_step(inner_state, gain_val), None
            end_state, _ = lax.scan(step_body, field_state, gain_row)
            return end_state, field_state

        u_final, checkpoints = lax.scan(fwd_segment, u_init, gain_rows)

        def back_segment(adj_carry, seg_inputs):
            start_state, gain_row = seg_inputs

            def rec_body(inner_state, gain_val):
                return fwd_step(inner_state, gain_val), inner_state
            last_state, early_states = lax.scan(rec_body, start_state, gain_row[:-1])
            seg_states = jnp.concatenate([early_states, last_state[None]], axis=0)

            def adj_body(step_carry, step_inputs):
                lam_next, grad_acc = step_carry
                field_state, gain_val = step_inputs
                grad_acc = grad_acc + gain_val * lam_next
                padded = exchange(lam_next, 1)
                lam_prev = stencil_apply(padded, flipped) + DT * (1.0 - 3.0 * field_state * field_state) * lam_next
                return (lam_prev, grad_acc), None

            adj_carry, _ = lax.scan(adj_body, adj_carry, (seg_states, gain_row), reverse=True)
            return adj_carry, None

        (grad_init, grad_forcing), _ = lax.scan(back_segment, (loss_weight, jnp.zeros_like(forcing)), (checkpoints, gain_rows), reverse=True)
        return u_final, grad_init, grad_forcing

    return jax.shard_map(local_run, mesh=mesh, in_specs=(field_spec, field_spec, field_spec, P(), P()), out_specs=(field_spec, field_spec, field_spec), check_vma=False)
```

profile of v0, /device:TPU:97, one launch (start us, length us, event | category | flops | bytes accessed | tf_op | source)
XLA Modules:
  0.0 1799.3 jit_solution(17665269759471203245)
XLA Ops:
  1.9 642.3 %while.104 = (s32[]{:T(128)}, f32[512,256]{1,0:T(8,128)S(1)}, f32[8,512,256]{2,1,0:T(8,128)}, f32[8,4]{1,0:T(8,128)S(1)}, f32[3,3]{1,0:T(4,128)S(1)}, /*index=5*...) while((s32[]{:T(128)}, f32[512,256]{1,0:T(8,128)S(1)}, ...), condition=%wide.region_3.4_spmd, body=%wide.region_0.3_spmd.sunk | while | flops 4463632 | bytes 9495230 | solution.py:62
  2.7 81.2 %while.108 = (s32[]{:T(128)}, f32[512,256]{1,0:T(8,128)S(1)}, f32[3,3]{1,0:T(4,128)S(1)}, f32[4]{0:T(128)S(1)}, f32[512,256]{1,0:T(8,128)S(1)}, /*index=5*/s32[]{:T(128)}) while((s32[]{:T(128)}, f32[512,256]{1,0:T(8,128)S(1)}, f32[3,3]{1,0:T(4,128)S(1)}, f32[4]{0:T(128)S(1)}, f32[512,256]{1,0:T(8,128)S(1)}, /*index=5*/s32[]{:T(128)}) %tuple.185), condition=%wide.region_2.2_spmd, body=%wide.region_1.1_spmd.sunk | while | flops 4463630 | bytes 8446441 | solution.py:59
  84.8 77.4 %while.108 = (s32[]{:T(128)}, f32[512,256]{1,0:T(8,128)S(1)}, f32[3,3]{1,0:T(4,128)S(1)}, f32[4]{0:T(128)S(1)}, f32[512,256]{1,0:T(8,128)S(1)}, /*index=5*/s32[]{:T(128)}) while((s32[]{:T(128)}, f32[512,256]{1,0:T(8,128)S(1)}, f32[3,3]{1,0:T(4,128)S(1)}, f32[4]{0:T(128)S(1)}, f32[512,256]{1,0:T(8,128)S(1)}, /*index=5*/s32[]{:T(128)}) %tuple.185), condition=%wide.region_2.2_spmd, body=%wide.region_1.1_spmd.sunk | while | flops 4463630 | bytes 8446441 | solution.py:59
  163.0 79.5 %while.108 = (s32[]{:T(128)}, f32[512,256]{1,0:T(8,128)S(1)}, f32[3,3]{1,0:T(4,128)S(1)}, f32[4]{0:T(128)S(1)}, f32[512,256]{1,0:T(8,128)S(1)}, /*index=5*/s32[]{:T(128)}) while((s32[]{:T(128)}, f32[512,256]{1,0:T(8,128)S(1)}, f32[3,3]{1,0:T(4,128)S(1)}, f32[4]{0:T(128)S(1)}, f32[512,256]{1,0:T(8,128)S(1)}, /*index=5*/s32[]{:T(128)}) %tuple.185), condition=%wide.region_2.2_spmd, body=%wide.region_1.1_spmd.sunk | while | flops 4463630 | bytes 8446441 | solution.py:59
  243.4 79.5 %while.108 = (s32[]{:T(128)}, f32[512,256]{1,0:T(8,128)S(1)}, f32[3,3]{1,0:T(4,128)S(1)}, f32[4]{0:T(128)S(1)}, f32[512,256]{1,0:T(8,128)S(1)}, /*index=5*/s32[]{:T(128)}) while((s32[]{:T(128)}, f32[512,256]{1,0:T(8,128)S(1)}, f32[3,3]{1,0:T(4,128)S(1)}, f32[4]{0:T(128)S(1)}, f32[512,256]{1,0:T(8,128)S(1)}, /*index=5*/s32[]{:T(128)}) %tuple.185), condition=%wide.region_2.2_spmd, body=%wide.region_1.1_spmd.sunk | while | flops 4463630 | bytes 8446441 | solution.py:59
  323.7 79.5 %while.108 = (s32[]{:T(128)}, f32[512,256]{1,0:T(8,128)S(1)}, f32[3,3]{1,0:T(4,128)S(1)}, f32[4]{0:T(128)S(1)}, f32[512,256]{1,0:T(8,128)S(1)}, /*index=5*/s32[]{:T(128)}) while((s32[]{:T(128)}, f32[512,256]{1,0:T(8,128)S(1)}, f32[3,3]{1,0:T(4,128)S(1)}, f32[4]{0:T(128)S(1)}, f32[512,256]{1,0:T(8,128)S(1)}, /*index=5*/s32[]{:T(128)}) %tuple.185), condition=%wide.region_2.2_spmd, body=%wide.region_1.1_spmd.sunk | while | flops 4463630 | bytes 8446441 | solution.py:59
  404.0 79.5 %while.108 = (s32[]{:T(128)}, f32[512,256]{1,0:T(8,128)S(1)}, f32[3,3]{1,0:T(4,128)S(1)}, f32[4]{0:T(128)S(1)}, f32[512,256]{1,0:T(8,128)S(1)}, /*index=5*/s32[]{:T(128)}) while((s32[]{:T(128)}, f32[512,256]{1,0:T(8,128)S(1)}, f32[3,3]{1,0:T(4,128)S(1)}, f32[4]{0:T(128)S(1)}, f32[512,256]{1,0:T(8,128)S(1)}, /*index=5*/s32[]{:T(128)}) %tuple.185), condition=%wide.region_2.2_spmd, body=%wide.region_1.1_spmd.sunk | while | flops 4463630 | bytes 8446441 | solution.py:59
  484.3 79.5 %while.108 = (s32[]{:T(128)}, f32[512,256]{1,0:T(8,128)S(1)}, f32[3,3]{1,0:T(4,128)S(1)}, f32[4]{0:T(128)S(1)}, f32[512,256]{1,0:T(8,128)S(1)}, /*index=5*/s32[]{:T(128)}) while((s32[]{:T(128)}, f32[512,256]{1,0:T(8,128)S(1)}, f32[3,3]{1,0:T(4,128)S(1)}, f32[4]{0:T(128)S(1)}, f32[512,256]{1,0:T(8,128)S(1)}, /*index=5*/s32[]{:T(128)}) %tuple.185), condition=%wide.region_2.2_spmd, body=%wide.region_1.1_spmd.sunk | while | flops 4463630 | bytes 8446441 | solution.py:59
  564.7 79.5 %while.108 = (s32[]{:T(128)}, f32[512,256]{1,0:T(8,128)S(1)}, f32[3,3]{1,0:T(4,128)S(1)}, f32[4]{0:T(128)S(1)}, f32[512,256]{1,0:T(8,128)S(1)}, /*index=5*/s32[]{:T(128)}) while((s32[]{:T(128)}, f32[512,256]{1,0:T(8,128)S(1)}, f32[3,3]{1,0:T(4,128)S(1)}, f32[4]{0:T(128)S(1)}, f32[512,256]{1,0:T(8,128)S(1)}, /*index=5*/s32[]{:T(128)}) %tuple.185), condition=%wide.region_2.2_spmd, body=%wide.region_1.1_spmd.sunk | while | flops 4463630 | bytes 8446441 | solution.py:59
  645.0 1153.4 %while.107 = (s32[]{:T(128)}, f32[512,256]{1,0:T(8,128)S(1)}, f32[512,256]{1,0:T(8,128)S(1)}, f32[8,512,256]{2,1,0:T(8,128)}, f32[8,4]{1,0:T(8,128)S(1)}, /*inde...) while((s32[]{:T(128)}, f32[512,256]{1,0:T(8,128)S(1)}, ...), condition=%wide.region_9.10_spmd, body=%wide.region_4.9_spmd.sunk | while | flops 9582624 | bytes 24757628 | solution.py:83
  646.1 59.7 %while.109 = (s32[]{:T(128)}, f32[512,256]{1,0:T(8,128)S(1)}, f32[3,512,256]{2,1,0:T(8,128)}, f32[3,3]{1,0:T(4,128)S(1)}, f32[3]{0:T(128)S(1)}, /*index=5*/f32[512,256]{1,0:T(8,128)S(1)}, s32[]{:T(128)}) while((s32[]{:T(128)}, f32[512,256]{1,0:T(8,128)S(1)}, f32[3,512,256]{2,1,0:T(8,128)}, f32[3,3]{1,0:T(4,128)S(1)}, f32[3]{0:T(128)S(1)}, ...), condition=%wide.region_6.6_spmd, body=%wide.region_5.5_spmd.sunk | while | flops 4463630 | bytes 9495029 | solution.py:69
  708.8 80.4 %while.110 = (s32[]{:T(128)}, f32[512,256]{1,0:T(8,128)S(1)}, f32[512,256]{1,0:T(8,128)S(1)}, f32[3,3]{1,0:T(4,128)S(1)}, f32[4,512,256]{2,1,0:T(8,128)}, /*index=5*/f32[4]{0:T(128)S(1)}, s32[]{:T(128)}, s32[]{:T(128)}) while((s32[]{:T(128)}, f32[512,256]{1,0:T(8,128)S(1)}, f32[512,256]{1,0:T(8,128)S(1)}, f32[3,3]{1,0:T(4,128)S(1)}, ...), condition=%wide.region_8.8_spmd, body=%wide.region_7.7_spmd.sunk | while | flops 4594703 | bytes 10019329 | solution.py:80
  790.3 59.8 %while.109 = (s32[]{:T(128)}, f32[512,256]{1,0:T(8,128)S(1)}, f32[3,512,256]{2,1,0:T(8,128)}, f32[3,3]{1,0:T(4,128)S(1)}, f32[3]{0:T(128)S(1)}, /*index=5*/f32[512,256]{1,0:T(8,128)S(1)}, s32[]{:T(128)}) while((s32[]{:T(128)}, f32[512,256]{1,0:T(8,128)S(1)}, f32[3,512,256]{2,1,0:T(8,128)}, f32[3,3]{1,0:T(4,128)S(1)}, f32[3]{0:T(128)S(1)}, ...), condition=%wide.region_6.6_spmd, body=%wide.region_5.5_spmd.sunk | while | flops 4463630 | bytes 9495029 | solution.py:69
  853.1 80.4 %while.110 = (s32[]{:T(128)}, f32[512,256]{1,0:T(8,128)S(1)}, f32[512,256]{1,0:T(8,128)S(1)}, f32[3,3]{1,0:T(4,128)S(1)}, f32[4,512,256]{2,1,0:T(8,128)}, /*index=5*/f32[4]{0:T(128)S(1)}, s32[]{:T(128)}, s32[]{:T(128)}) while((s32[]{:T(128)}, f32[512,256]{1,0:T(8,128)S(1)}, f32[512,256]{1,0:T(8,128)S(1)}, f32[3,3]{1,0:T(4,128)S(1)}, ...), condition=%wide.region_8.8_spmd, body=%wide.region_7.7_spmd.sunk | while | flops 4594703 | bytes 10019329 | solution.py:80
  934.6 59.8 %while.109 = (s32[]{:T(128)}, f32[512,256]{1,0:T(8,128)S(1)}, f32[3,512,256]{2,1,0:T(8,128)}, f32[3,3]{1,0:T(4,128)S(1)}, f32[3]{0:T(128)S(1)}, /*index=5*/f32[512,256]{1,0:T(8,128)S(1)}, s32[]{:T(128)}) while((s32[]{:T(128)}, f32[512,256]{1,0:T(8,128)S(1)}, f32[3,512,256]{2,1,0:T(8,128)}, f32[3,3]{1,0:T(4,128)S(1)}, f32[3]{0:T(128)S(1)}, ...), condition=%wide.region_6.6_spmd, body=%wide.region_5.5_spmd.sunk | while | flops 4463630 | bytes 9495029 | solution.py:69
  997.5 80.4 %while.110 = (s32[]{:T(128)}, f32[512,256]{1,0:T(8,128)S(1)}, f32[512,256]{1,0:T(8,128)S(1)}, f32[3,3]{1,0:T(4,128)S(1)}, f32[4,512,256]{2,1,0:T(8,128)}, /*index=5*/f32[4]{0:T(128)S(1)}, s32[]{:T(128)}, s32[]{:T(128)}) while((s32[]{:T(128)}, f32[512,256]{1,0:T(8,128)S(1)}, f32[512,256]{1,0:T(8,128)S(1)}, f32[3,3]{1,0:T(4,128)S(1)}, ...), condition=%wide.region_8.8_spmd, body=%wide.region_7.7_spmd.sunk | while | flops 4594703 | bytes 10019329 | solution.py:80
  1141.2 80.4 %while.110 = (s32[]{:T(128)}, f32[512,256]{1,0:T(8,128)S(1)}, f32[512,256]{1,0:T(8,128)S(1)}, f32[3,3]{1,0:T(4,128)S(1)}, f32[4,512,256]{2,1,0:T(8,128)}, /*index=5*/f32[4]{0:T(128)S(1)}, s32[]{:T(128)}, s32[]{:T(128)}) while((s32[]{:T(128)}, f32[512,256]{1,0:T(8,128)S(1)}, f32[512,256]{1,0:T(8,128)S(1)}, f32[3,3]{1,0:T(4,128)S(1)}, ...), condition=%wide.region_8.8_spmd, body=%wide.region_7.7_spmd.sunk | while | flops 4594703 | bytes 10019329 | solution.py:80
  1222.7 59.8 %while.109 = (s32[]{:T(128)}, f32[512,256]{1,0:T(8,128)S(1)}, f32[3,512,256]{2,1,0:T(8,128)}, f32[3,3]{1,0:T(4,128)S(1)}, f32[3]{0:T(128)S(1)}, /*index=5*/f32[512,256]{1,0:T(8,128)S(1)}, s32[]{:T(128)}) while((s32[]{:T(128)}, f32[512,256]{1,0:T(8,128)S(1)}, f32[3,512,256]{2,1,0:T(8,128)}, f32[3,3]{1,0:T(4,128)S(1)}, f32[3]{0:T(128)S(1)}, ...), condition=%wide.region_6.6_spmd, body=%wide.region_5.5_spmd.sunk | while | flops 4463630 | bytes 9495029 | solution.py:69
  1285.5 80.4 %while.110 = (s32[]{:T(128)}, f32[512,256]{1,0:T(8,128)S(1)}, f32[512,256]{1,0:T(8,128)S(1)}, f32[3,3]{1,0:T(4,128)S(1)}, f32[4,512,256]{2,1,0:T(8,128)}, /*index=5*/f32[4]{0:T(128)S(1)}, s32[]{:T(128)}, s32[]{:T(128)}) while((s32[]{:T(128)}, f32[512,256]{1,0:T(8,128)S(1)}, f32[512,256]{1,0:T(8,128)S(1)}, f32[3,3]{1,0:T(4,128)S(1)}, ...), condition=%wide.region_8.8_spmd, body=%wide.region_7.7_spmd.sunk | while | flops 4594703 | bytes 10019329 | solution.py:80
  1367.1 59.8 %while.109 = (s32[]{:T(128)}, f32[512,256]{1,0:T(8,128)S(1)}, f32[3,512,256]{2,1,0:T(8,128)}, f32[3,3]{1,0:T(4,128)S(1)}, f32[3]{0:T(128)S(1)}, /*index=5*/f32[512,256]{1,0:T(8,128)S(1)}, s32[]{:T(128)}) while((s32[]{:T(128)}, f32[512,256]{1,0:T(8,128)S(1)}, f32[3,512,256]{2,1,0:T(8,128)}, f32[3,3]{1,0:T(4,128)S(1)}, f32[3]{0:T(128)S(1)}, ...), condition=%wide.region_6.6_spmd, body=%wide.region_5.5_spmd.sunk | while | flops 4463630 | bytes 9495029 | solution.py:69
  1429.9 80.4 %while.110 = (s32[]{:T(128)}, f32[512,256]{1,0:T(8,128)S(1)}, f32[512,256]{1,0:T(8,128)S(1)}, f32[3,3]{1,0:T(4,128)S(1)}, f32[4,512,256]{2,1,0:T(8,128)}, /*index=5*/f32[4]{0:T(128)S(1)}, s32[]{:T(128)}, s32[]{:T(128)}) while((s32[]{:T(128)}, f32[512,256]{1,0:T(8,128)S(1)}, f32[512,256]{1,0:T(8,128)S(1)}, f32[3,3]{1,0:T(4,128)S(1)}, ...), condition=%wide.region_8.8_spmd, body=%wide.region_7.7_spmd.sunk | while | flops 4594703 | bytes 10019329 | solution.py:80
  1511.4 59.8 %while.109 = (s32[]{:T(128)}, f32[512,256]{1,0:T(8,128)S(1)}, f32[3,512,256]{2,1,0:T(8,128)}, f32[3,3]{1,0:T(4,128)S(1)}, f32[3]{0:T(128)S(1)}, /*index=5*/f32[512,256]{1,0:T(8,128)S(1)}, s32[]{:T(128)}) while((s32[]{:T(128)}, f32[512,256]{1,0:T(8,128)S(1)}, f32[3,512,256]{2,1,0:T(8,128)}, f32[3,3]{1,0:T(4,128)S(1)}, f32[3]{0:T(128)S(1)}, ...), condition=%wide.region_6.6_spmd, body=%wide.region_5.5_spmd.sunk | while | flops 4463630 | bytes 9495029 | solution.py:69
  1574.2 80.4 %while.110 = (s32[]{:T(128)}, f32[512,256]{1,0:T(8,128)S(1)}, f32[512,256]{1,0:T(8,128)S(1)}, f32[3,3]{1,0:T(4,128)S(1)}, f32[4,512,256]{2,1,0:T(8,128)}, /*index=5*/f32[4]{0:T(128)S(1)}, s32[]{:T(128)}, s32[]{:T(128)}) while((s32[]{:T(128)}, f32[512,256]{1,0:T(8,128)S(1)}, f32[512,256]{1,0:T(8,128)S(1)}, f32[3,3]{1,0:T(4,128)S(1)}, ...), condition=%wide.region_8.8_spmd, body=%wide.region_7.7_spmd.sunk | while | flops 4594703 | bytes 10019329 | solution.py:80
  1718.0 80.4 %while.110 = (s32[]{:T(128)}, f32[512,256]{1,0:T(8,128)S(1)}, f32[512,256]{1,0:T(8,128)S(1)}, f32[3,3]{1,0:T(4,128)S(1)}, f32[4,512,256]{2,1,0:T(8,128)}, /*index=5*/f32[4]{0:T(128)S(1)}, s32[]{:T(128)}, s32[]{:T(128)}) while((s32[]{:T(128)}, f32[512,256]{1,0:T(8,128)S(1)}, f32[512,256]{1,0:T(8,128)S(1)}, f32[3,3]{1,0:T(4,128)S(1)}, ...), condition=%wide.region_8.8_spmd, body=%wide.region_7.7_spmd.sunk | while | flops 4594703 | bytes 10019329 | solution.py:80
  (1550 shorter events, 1910.7 us)
Async XLA Ops:
  167.4 8.5 collective-permute-start.10
  167.5 8.5 collective-permute-start.11
  247.7 8.5 collective-permute-start.10
  247.8 8.5 collective-permute-start.11
  328.1 8.5 collective-permute-start.10
  328.1 8.5 collective-permute-start.11
  408.4 8.5 collective-permute-start.10
  488.7 8.5 collective-permute-start.10
  569.1 8.5 collective-permute-start.10
  650.5 8.6 collective-permute-start.2
  650.5 8.5 collective-permute-start.3
  733.0 8.5 collective-permute-start.7
  814.5 8.5 collective-permute-start.2
  814.6 8.5 collective-permute-start.3
  897.4 8.5 collective-permute-start.7
  978.6 8.5 collective-permute-start.2
  1061.7 8.5 collective-permute-start.7
  1227.1 8.7 collective-permute-start.2
  1227.2 8.6 collective-permute-start.3
  1309.8 8.5 collective-permute-start.7
  1391.3 8.5 collective-permute-start.2
  1474.1 8.5 collective-permute-start.7
  1555.3 8.5 collective-permute-start.2
  1638.4 8.5 collective-permute-start.7
  (336 other events, 2429.3 us)
where the time goes:
time: 1810 us; the launch traced here: 1800 us
  starting transfers between devices  741 us (41%)
  other arithmetic  709 us (39%)
  waiting for transfers between devices  178 us (10%)
  local copies, waits for them, and re-layouts  165 us (9%)
    ppermute x88, starting transfers between devices, exchange(): from_right = lax.ppermute(tall_tile[:, :halo_depth], col_axes, to_prev_col)  586 us
    add x56, other arithmetic, fwd_step(): stencil_apply(padded, weights)  396 us
    add x32, other arithmetic, adj_body(): stencil_apply(padded, flipped)  235 us
    ppermute x88, starting transfers between devices, exchange(): from_above = lax.ppermute(tile_vals[-halo_depth:], 'row', to_next_row)  117 us
    ppermute x88, waiting for transfers between devices, exchange(): from_above = lax.ppermute(tile_vals[-halo_depth:], 'row', to_next_row)  112 us
    slice x88, local copies, waits for them, and re-layouts, stencil_apply(): weights[row_off, col_off]  59.8 us
    dynamic_slice x64, local copies, waits for them, and re-layouts, fwd_segment(): end_state, _ = lax.scan(step_body, field_state, gain_row)  37.5 us
  transfers between devices with their start and end apart: 352, of which 216 were waited for; matrix products, arithmetic and copies ran while one was open for 9% of the time, Pallas kernels for 0%

commit v1 on v0

v1 whole, which is shorter than its diff:
```python
import functools

import jax
import jax.numpy as jnp
from jax import lax
from jax.experimental import pallas as pl
from jax.experimental.pallas import tpu as pltpu
from jax.sharding import PartitionSpec as P


DT = 0.01
LANES = 128
PHASE = 8
UNROLL = 8
MESH = pl.DeviceIdType.MESH


def stencil_blocks(load, wts, centre, nb):
    part = {}
    for b in range(nb):
        left, mid, right = load(b, -1), load(b, 0), load(b, 1)
        part[b, -1] = (wts[0][0] * left + wts[0][1] * mid) + wts[0][2] * right
        part[b, 0] = (wts[1][0] * left + centre(b, mid) * mid) + wts[1][2] * right
        part[b, 1] = (wts[2][0] * left + wts[2][1] * mid) + wts[2][2] * right
    part[-1, -1] = pltpu.roll(part[nb - 1, -1], 1, 1)
    part[nb, 1] = pltpu.roll(part[0, 1], LANES - 1, 1)
    return [(part[b - 1, -1] + part[b, 0]) + part[b + 1, 1] for b in range(nb)]


def kernel(row_size, col_size, core_size, tiles, wts_ref, gains_ref, u_hbm, f_hbm, w_hbm, uo_hbm, go_hbm, gf_hbm,
           nat, ring, lam, coef, force, acc, loc_sem, row_send, row_recv, f_send, f_recv,
           u_send, u_recv, l_send, l_recv, out_sem):
    rows, width, steps = tiles
    nb = force.shape[0]
    halo = (nb * LANES - rows) // 2
    half = halo // 2
    fdep, adep = 2 * PHASE, PHASE
    org = fdep
    phases = steps // PHASE
    groups = width // 8
    scale = DT ** 0.5

    row_id, col_id, core_id = lax.axis_index("row"), lax.axis_index("col"), lax.axis_index("core")
    up, down = lax.rem(row_id + row_size - 1, row_size), lax.rem(row_id + 1, row_size)
    flat = col_id * core_size + core_id
    total = col_size * core_size
    lflat, rflat = lax.rem(flat + total - 1, total), lax.rem(flat + 1, total)
    above, below = {"row": up}, {"row": down}
    left = {"col": lax.div(lflat, core_size), "core": lax.rem(lflat, core_size)}
    right = {"col": lax.div(rflat, core_size), "core": lax.rem(rflat, core_size)}

    srcs = (u_hbm, f_hbm, w_hbm)
    cblocks = width // LANES
    local = [[pltpu.make_async_copy(srcs[k].at[:, pl.ds(cb * LANES, LANES)], nat.at[k, cb, pl.ds(halo, rows), :],
                                    loc_sem.at[k, cb]) for cb in range(cblocks)] for k in range(3)]
    for k in range(2):
        for copy in local[k]:
            copy.start()

    barrier = pltpu.get_barrier_semaphore()
    for dev in (above, below, left, right):
        pl.semaphore_signal(barrier, inc=1, device_id=dev, device_id_type=MESH)
    pl.semaphore_wait(barrier, 4)

    def row_copies(k):
        dep = halo if k < 2 else half
        out = []
        for cb in range(cblocks):
            lanes = pl.ds(cb * LANES, LANES)
            out.append(pltpu.make_async_remote_copy(
                srcs[k].at[pl.ds(0, dep), lanes], nat.at[k, cb, pl.ds(halo + rows, dep), :],
                row_send.at[k, cb, 0], row_recv.at[k, cb, 0], device_id=above, device_id_type=MESH))
            out.append(pltpu.make_async_remote_copy(
                srcs[k].at[pl.ds(rows - dep, dep), lanes], nat.at[k, cb, pl.ds(halo - dep, dep), :],
                row_send.at[k, cb, 1], row_recv.at[k, cb, 1], device_id=below, device_id_type=MESH))
        return out

    def col_copies(ref, dep, send, recv):
        return [
            pltpu.make_async_remote_copy(ref.at[:, pl.ds(org, dep), :], ref.at[:, pl.ds(org + width, dep), :],
                                         send.at[0], recv.at[0], device_id=left, device_id_type=MESH),
            pltpu.make_async_remote_copy(ref.at[:, pl.ds(org + width - dep, dep), :], ref.at[:, pl.ds(org - dep, dep), :],
                                         send.at[1], recv.at[1], device_id=right, device_id_type=MESH),
        ]

    rcopies = [row_copies(k) for k in range(3)]
    for k in range(2):
        for copy in rcopies[k]:
            copy.start()
    for copy in local[2]:
        copy.start()
    for copy in rcopies[2]:
        copy.start()

    def arrive(k, dst, factor):
        for copy in local[k]:
            copy.wait()
        for copy in rcopies[k]:
            copy.wait()
        for cb in range(cblocks):
            for b in range(nb):
                val = jnp.transpose(nat[k, cb, pl.ds(b, LANES, stride=nb), :])
                if factor is not None:
                    val = val * factor
                dst[b, pl.ds(org + cb * LANES, LANES), :] = val

    def depart(src, k, out, factor):
        for cb in range(cblocks):
            for b in range(nb):
                val = jnp.transpose(src[b, pl.ds(org + cb * LANES, LANES), :])
                if factor is not None:
                    val = val * factor
                nat[k, cb, pl.ds(b, LANES, stride=nb), :] = val
        return [pltpu.make_async_copy(nat.at[k, cb, pl.ds(halo, rows), :], out.at[:, pl.ds(cb * LANES, LANES)],
                                      out_sem.at[k, cb]) for cb in range(cblocks)]

    arrive(0, ring.at[0], scale)
    for copy in col_copies(ring.at[0], fdep, u_send.at[0], u_recv.at[0]):
        copy.start()
    arrive(1, force, scale)
    fcopies = col_copies(force, fdep, f_send, f_recv)
    for copy in fcopies:
        copy.start()

    wts = [[wts_ref[i, j] for j in range(3)] for i in range(3)]
    flip = [[wts_ref[2 - i, 2 - j] for j in range(3)] for i in range(3)]
    mid_wt = wts_ref[1, 1] + DT

    def sweep(body, base, count):
        full, rest = divmod(count, UNROLL)
        if full == 1:
            body(base, 8 * UNROLL)
        elif full > 1:
            def block(i, _):
                body(base + i * (8 * UNROLL), 8 * UNROLL)
                return 0
            lax.fori_loop(0, full, block, 0)
        if rest:
            body(base + full * 8 * UNROLL, 8 * rest)

    def cover(step_body, dep):
        def middle():
            for j in range(1, PHASE + 1):
                sweep(functools.partial(step_body, j), org + j, groups - j)

        def sides():
            for j in range(1, PHASE):
                sweep(functools.partial(step_body, j), org + j - dep, dep // 8)
                sweep(functools.partial(step_body, j), org + width - 7 * j, -(-(dep + 6 * j) // 8))
            sweep(functools.partial(step_body, PHASE), org, PHASE // 8)
            sweep(functools.partial(step_body, PHASE), org + width - 7 * PHASE, 7 * PHASE // 8)
        return middle, sides

    def slot(phase, j):
        return lax.rem(phase * PHASE + j, 2 * PHASE)

    def reaction(val, t, b, at):
        sq = val * val
        weight = mid_wt - sq
        coef[t, b, at, :] = (weight - sq) - sq
        return weight

    def fwd_phase(phase, _):
        def step_body(j, base, cols):
            src, dst, t = slot(phase, j - 1), slot(phase, j), phase * PHASE + (j - 1)
            gain = gains_ref[t]
            at = pl.ds(base, cols)

            def centre(b, mid):
                return reaction(mid, t, b, at)
            sums = stencil_blocks(lambda b, d: ring[src, b, pl.ds(base + d, cols), :], wts, centre, nb)
            for b in range(nb):
                ring[dst, b, at, :] = sums[b] + gain * force[b, at, :]

        par = lax.rem(phase, 2)
        middle, sides = cover(step_body, fdep)
        middle()
        for copy in col_copies(ring.at[slot(phase, 0)], fdep, u_send.at[par], u_recv.at[par]):
            copy.wait()

        @pl.when(phase == 0)
        def _():
            for copy in fcopies:
                copy.wait()
        sides()
        last = phase * PHASE + (PHASE - 1)
        for at in (pl.ds(org - PHASE, PHASE), pl.ds(org + width, PHASE)):
            for b in range(nb):
                reaction(ring[slot(phase, PHASE - 1), b, at, :], last, b, at)

        @pl.when(phase < phases - 1)
        def _():
            for copy in col_copies(ring.at[slot(phase, PHASE)], fdep, u_send.at[1 - par], u_recv.at[1 - par]):
                copy.start()
        return 0

    lax.fori_loop(0, phases, fwd_phase, 0)

    arrive(2, lam.at[0], None)
    for copy in col_copies(lam.at[0], adep, l_send.at[0], l_recv.at[0]):
        copy.start()
    ucopies = depart(ring.at[(phases % 2) * PHASE], 0, uo_hbm, 1.0 / scale)
    for copy in ucopies:
        copy.start()
    acc[...] = jnp.zeros_like(acc)

    def adj_phase(phase, _):
        def step_body(j, base, cols):
            src, dst, t = slot(phase, j - 1), slot(phase, j), steps - (phase * PHASE + j)
            gain = gains_ref[t]
            at = pl.ds(base, cols)

            def centre(b, mid):
                acc[b, at, :] += gain * mid
                return coef[t, b, at, :]
            sums = stencil_blocks(lambda b, d: lam[src, b, pl.ds(base + d, cols), :], flip, centre, nb)
            for b in range(nb):
                lam[dst, b, at, :] = sums[b]

        par = lax.rem(phase, 2)
        middle, sides = cover(step_body, adep)
        middle()
        for copy in col_copies(lam.at[slot(phase, 0)], adep, l_send.at[par], l_recv.at[par]):
            copy.wait()
        sides()

        @pl.when(phase < phases - 1)
        def _():
            for copy in col_copies(lam.at[slot(phase, PHASE)], adep, l_send.at[1 - par], l_recv.at[1 - par]):
                copy.start()
        return 0

    lax.fori_loop(0, phases, adj_phase, 0)

    gcopies = depart(lam.at[(phases % 2) * PHASE], 1, go_hbm, None)
    for copy in gcopies:
        copy.start()
    fo_copies = depart(acc, 2, gf_hbm, None)
    for copy in fo_copies:
        copy.start()
    for copy in ucopies + gcopies + fo_copies:
        copy.wait()


def solution(mesh):
    row_size, col_size, core_size = mesh.shape["row"], mesh.shape["col"], mesh.shape["core"]
    field_spec = P(("mem", "row"), ("col", "core"))

    def local_run(u_init, forcing, loss_weight, weights, gains):
        rows, width = u_init.shape
        steps = gains.shape[0]
        nb = -(-(rows + 4 * steps) // LANES)
        cols = width + 4 * PHASE + 8
        cblocks = width // LANES
        f32 = jnp.float32
        field = (nb, cols, LANES)
        dma = pltpu.SemaphoreType.DMA
        hbm, smem = pl.BlockSpec(memory_space=pl.ANY), pl.BlockSpec(memory_space=pltpu.SMEM)
        return pl.pallas_call(
            functools.partial(kernel, row_size, col_size, core_size, (rows, width, steps)),
            out_shape=[jax.ShapeDtypeStruct((rows, width), f32)] * 3,
            in_specs=[smem, smem, hbm, hbm, hbm],
            out_specs=[hbm, hbm, hbm],
            scratch_shapes=[
                pltpu.VMEM((3, cblocks, nb * LANES, LANES), f32),
                pltpu.VMEM((2 * PHASE,) + field, f32),
                pltpu.VMEM((2 * PHASE,) + field, f32),
                pltpu.VMEM((steps,) + field, f32),
                pltpu.VMEM(field, f32),
                pltpu.VMEM(field, f32),
                dma((3, cblocks)),
                dma((3, cblocks, 2)),
                dma((3, cblocks, 2)),
                dma((2,)),
                dma((2,)),
                dma((2, 2)),
                dma((2, 2)),
                dma((2, 2)),
                dma((2, 2)),
                dma((3, cblocks)),
            ],
            compiler_params=pltpu.CompilerParams(
                collective_id=0, has_side_effects=True, vmem_limit_bytes=60 * 1024 * 1024),
            name="steps",
        )(weights, gains, u_init, forcing, loss_weight)

    return jax.shard_map(local_run, mesh=mesh, in_specs=(field_spec, field_spec, field_spec, P(), P()),
                         out_specs=(field_spec, field_spec, field_spec), check_vma=False)
```

time: 1810 us -> 56.9 us (0.03)
  starting transfers between devices: 741 us -> 0 us
  other arithmetic: 709 us -> 0 us
  waiting for transfers between devices: 178 us -> 0 us
  local copies, waits for them, and re-layouts: 165 us -> 3.95 us
  Pallas kernels: 0 us -> 51.7 us
    ppermute x352 -> x0, starting transfers between devices: 741 us -> none  [the longest x88 586 us: exchange(): from_right = lax.ppermute(tall_tile[:, :halo_depth], col_axes, to_prev_col)]
    add x120 -> x0, other arithmetic: 655 us -> none  [the longest x56 396 us: fwd_step(): stencil_apply(padded, weights)]
    ppermute x352 -> x0, waiting for transfers between devices: 178 us -> none  [the longest x88 112 us: exchange(): from_above = lax.ppermute(tile_vals[-halo_depth:], 'row', to_next_row)]
    slice x272 -> x0, local copies, waits for them, and re-layouts: 71.5 us -> none  [the longest x88 59.8 us: stencil_apply(): weights[row_off, col_off]]
    concatenate x184 -> x0, other arithmetic: 53.2 us -> none  [the longest x88 25.8 us: exchange(): return jnp.concatenate([from_left, tall_tile, from_right], axis=1)]
    dynamic_slice x96 -> x0, local copies, waits for them, and re-layouts: 52.1 us -> none  [the longest x64 37.5 us: fwd_segment(): end_state, _ = lax.scan(step_body, field_state, gain_row)]
    pallas_call x0 -> x1, Pallas kernels: none -> 51.7 us  [local_run(): pl.pallas_call(functools.partial(kernel, row_size, col_size, core_size, (...]
    dynamic_update_slice x32 -> x0, local copies, waits for them, and re-layouts: 26.8 us -> none  [the longest x24 20.1 us: back_segment(): last_state, early_states = lax.scan(rec_body, start_state, gain_row[:-1])]
  transfers between devices with their start and end apart: 352 -> 0, of which waited for: 216 -> 0; matrix products, arithmetic and copies ran while one was open for 9% -> 0% of each run, Pallas kernels for 0% -> 0%
where the time goes in v1:
time: 56.9 us; the launch traced here: 56.3 us
  Pallas kernels  51.7 us (91%)
  local copies, waits for them, and re-layouts  3.95 us (7%)
  between operations  0.65 us (1%)
    pallas_call x1, Pallas kernels, local_run(): pl.pallas_call(functools.partial(kernel, row_size, col_size, core_size, (...  51.7 us
    unnamed x7, local copies, waits for them, and re-layouts  3.95 us

profile of v1, /device:TPU:97, one launch (start us, length us, event | category | flops | bytes accessed | tf_op | source)
XLA Modules:
  0.0 56.3 jit_solution(14872475792470166589)
XLA Ops:
  0.6 51.7 %steps.1 = (f32[512,256]{1,0:T(8,128)}, f32[512,256]{1,0:T(8,128)}, f32[512,256]{1,0:T(8,128)}) custom-call(f32[3,3]{1,0:T(4,128)} %wts_ref.1, f32[32]{0:T(128)} %gains_ref.1, f32[512,256]{1,0:T(8,128)} %u_hbm.1, f32[512,256]{1,0:T(8,128)} %f_hbm.1, f32[512,256]{1,0:T(8,128)} %w_hbm.1), custom_call_target="tpu_custom_call" | custom-call | tf_op jit(solution)/shard_map/steps/pallas_call | solution.py:259
  52.3 0.0 copy-start.1
  52.3 1.9 %copy.11 = f32[512,256]{1,0:T(8,128)} copy(f32[512,256]{1,0:T(8,128)} %get-tuple-element.6) | data formatting | bytes 1048576
  54.3 0.0 copy-done.1
  54.3 0.0 copy-start
  54.3 0.8 %copy.12 = f32[512,256]{1,0:T(8,128)} copy(f32[512,256]{1,0:T(8,128)S(1)} %copy-done.1) | data formatting | bytes 1048576
  55.1 0.4 copy-done
  55.5 0.8 %copy.13 = f32[512,256]{1,0:T(8,128)} copy(f32[512,256]{1,0:T(8,128)S(1)} %copy-done) | data formatting | bytes 1048576
Async XLA Ops:
  52.3 1.9 %copy-start.1 = (f32[512,256]{1,0:T(8,128)S(1)}, f32[512,256]{1,0:T(8,128)}, u32[]{:S(2)}) copy-start(f32[512,256]{1,0:T(8,128)} %get-tuple-element.7) | copy-start | bytes 1572868
  54.3 1.2 %copy-start = (f32[512,256]{1,0:T(8,128)S(1)}, f32[512,256]{1,0:T(8,128)}, u32[]{:S(2)}) copy-start(f32[512,256]{1,0:T(8,128)} %get-tuple-element.8) | copy-start | bytes 1572868

commit v2 on v1

--- a/solution.py
+++ b/solution.py
@@ -28,7 +28,7 @@
 
 
 def kernel(row_size, col_size, core_size, tiles, wts_ref, gains_ref, u_hbm, f_hbm, w_hbm, uo_hbm, go_hbm, gf_hbm,
-           nat, ring, lam, coef, force, acc, loc_sem, row_send, row_recv, f_send, f_recv,
+           nat, ubase, lbase, inner, coef, force, acc, loc_sem, row_send, row_recv, f_send, f_recv,
            u_send, u_recv, l_send, l_recv, out_sem):
     rows, width, steps = tiles
     nb = force.shape[0]
@@ -114,8 +114,8 @@
         return [pltpu.make_async_copy(nat.at[k, cb, pl.ds(halo, rows), :], out.at[:, pl.ds(cb * LANES, LANES)],
                                       out_sem.at[k, cb]) for cb in range(cblocks)]
 
-    arrive(0, ring.at[0], scale)
-    for copy in col_copies(ring.at[0], fdep, u_send.at[0], u_recv.at[0]):
+    arrive(0, ubase.at[0], scale)
+    for copy in col_copies(ubase.at[0], fdep, u_send.at[0], u_recv.at[0]):
         copy.start()
     arrive(1, force, scale)
     fcopies = col_copies(force, fdep, f_send, f_recv)
@@ -151,8 +151,10 @@
             sweep(functools.partial(step_body, PHASE), org + width - 7 * PHASE, 7 * PHASE // 8)
         return middle, sides
 
-    def slot(phase, j):
-        return lax.rem(phase * PHASE + j, 2 * PHASE)
+    def level(base, par, j):
+        if j == 0:
+            return base.at[par]
+        return base.at[1 - par] if j == PHASE else inner.at[j - 1]
 
     def reaction(val, t, b, at):
         sq = val * val
@@ -161,21 +163,22 @@
         return weight
 
     def fwd_phase(phase, _):
+        par = lax.rem(phase, 2)
+
         def step_body(j, base, cols):
-            src, dst, t = slot(phase, j - 1), slot(phase, j), phase * PHASE + (j - 1)
+            src, dst, t = level(ubase, par, j - 1), level(ubase, par, j), phase * PHASE + (j - 1)
             gain = gains_ref[t]
             at = pl.ds(base, cols)
 
             def centre(b, mid):
                 return reaction(mid, t, b, at)
-            sums = stencil_blocks(lambda b, d: ring[src, b, pl.ds(base + d, cols), :], wts, centre, nb)
-            for b in range(nb):
-                ring[dst, b, at, :] = sums[b] + gain * force[b, at, :]
-
-        par = lax.rem(phase, 2)
+            sums = stencil_blocks(lambda b, d: src[b, pl.ds(base + d, cols), :], wts, centre, nb)
+            for b in range(nb):
+                dst[b, at, :] = sums[b] + gain * force[b, at, :]
+
         middle, sides = cover(step_body, fdep)
         middle()
-        for copy in col_copies(ring.at[slot(phase, 0)], fdep, u_send.at[par], u_recv.at[par]):
+        for copy in col_copies(ubase.at[par], fdep, u_send.at[par], u_recv.at[par]):
             copy.wait()
 
         @pl.when(phase == 0)
@@ -186,53 +189,54 @@
         last = phase * PHASE + (PHASE - 1)
         for at in (pl.ds(org - PHASE, PHASE), pl.ds(org + width, PHASE)):
             for b in range(nb):
-                reaction(ring[slot(phase, PHASE - 1), b, at, :], last, b, at)
+                reaction(inner[PHASE - 2, b, at, :], last, b, at)
 
         @pl.when(phase < phases - 1)
         def _():
-            for copy in col_copies(ring.at[slot(phase, PHASE)], fdep, u_send.at[1 - par], u_recv.at[1 - par]):
+            for copy in col_copies(ubase.at[1 - par], fdep, u_send.at[1 - par], u_recv.at[1 - par]):
                 copy.start()
         return 0
 
     lax.fori_loop(0, phases, fwd_phase, 0)
 
-    arrive(2, lam.at[0], None)
-    for copy in col_copies(lam.at[0], adep, l_send.at[0], l_recv.at[0]):
-        copy.start()
-    ucopies = depart(ring.at[(phases % 2) * PHASE], 0, uo_hbm, 1.0 / scale)
+    arrive(2, lbase.at[0], None)
+    for copy in col_copies(lbase.at[0], adep, l_send.at[0], l_recv.at[0]):
+        copy.start()
+    ucopies = depart(ubase.at[phases % 2], 0, uo_hbm, 1.0 / scale)
     for copy in ucopies:
         copy.start()
     acc[...] = jnp.zeros_like(acc)
 
     def adj_phase(phase, _):
+        par = lax.rem(phase, 2)
+
         def step_body(j, base, cols):
-            src, dst, t = slot(phase, j - 1), slot(phase, j), steps - (phase * PHASE + j)
+            src, dst, t = level(lbase, par, j - 1), level(lbase, par, j), steps - (phase * PHASE + j)
             gain = gains_ref[t]
             at = pl.ds(base, cols)
 
             def centre(b, mid):
                 acc[b, at, :] += gain * mid
                 return coef[t, b, at, :]
-            sums = stencil_blocks(lambda b, d: lam[src, b, pl.ds(base + d, cols), :], flip, centre, nb)
-            for b in range(nb):
-                lam[dst, b, at, :] = sums[b]
-
-        par = lax.rem(phase, 2)
+            sums = stencil_blocks(lambda b, d: src[b, pl.ds(base + d, cols), :], flip, centre, nb)
+            for b in range(nb):
+                dst[b, at, :] = sums[b]
+
         middle, sides = cover(step_body, adep)
         middle()
-        for copy in col_copies(lam.at[slot(phase, 0)], adep, l_send.at[par], l_recv.at[par]):
+        for copy in col_copies(lbase.at[par], adep, l_send.at[par], l_recv.at[par]):
             copy.wait()
         sides()
 
         @pl.when(phase < phases - 1)
         def _():
-            for copy in col_copies(lam.at[slot(phase, PHASE)], adep, l_send.at[1 - par], l_recv.at[1 - par]):
+            for copy in col_copies(lbase.at[1 - par], adep, l_send.at[1 - par], l_recv.at[1 - par]):
                 copy.start()
         return 0
 
     lax.fori_loop(0, phases, adj_phase, 0)
 
-    gcopies = depart(lam.at[(phases % 2) * PHASE], 1, go_hbm, None)
+    gcopies = depart(lbase.at[phases % 2], 1, go_hbm, None)
     for copy in gcopies:
         copy.start()
     fo_copies = depart(acc, 2, gf_hbm, None)
@@ -263,8 +267,9 @@
             out_specs=[hbm, hbm, hbm],
             scratch_shapes=[
                 pltpu.VMEM((3, cblocks, nb * LANES, LANES), f32),
-                pltpu.VMEM((2 * PHASE,) + field, f32),
-                pltpu.VMEM((2 * PHASE,) + field, f32),
+                pltpu.VMEM((2,) + field, f32),
+                pltpu.VMEM((2,) + field, f32),
+                pltpu.VMEM((PHASE - 1,) + field, f32),
                 pltpu.VMEM((steps,) + field, f32),
                 pltpu.VMEM(field, f32),
                 pltpu.VMEM(field, f32),

time: 56.9 us -> 53.6 us (0.942)
  Pallas kernels: 51.7 us -> 48.4 us
    pallas_call x1, Pallas kernels: 51.7 us -> 48.4 us  [local_run(): pl.pallas_call(functools.partial(kernel, row_size, col_size, core_size, (...]
where the time goes in v2:
time: 53.6 us; the launch traced here: 53 us
  Pallas kernels  48.4 us (90%)
  local copies, waits for them, and re-layouts  3.95 us (7%)
  between operations  0.65 us (1%)
    pallas_call x1, Pallas kernels, local_run(): pl.pallas_call(functools.partial(kernel, row_size, col_size, core_size, (...  48.4 us
    unnamed x7, local copies, waits for them, and re-layouts  3.95 us

profile of v2, /device:TPU:97, one launch (start us, length us, event | category | flops | bytes accessed | tf_op | source)
XLA Modules:
  0.0 53.0 jit_solution(4949488301894682010)
XLA Ops:
  0.6 48.4 %steps.1 = (f32[512,256]{1,0:T(8,128)}, f32[512,256]{1,0:T(8,128)}, f32[512,256]{1,0:T(8,128)}) custom-call(f32[3,3]{1,0:T(4,128)} %wts_ref.1, f32[32]{0:T(128)} %gains_ref.1, f32[512,256]{1,0:T(8,128)} %u_hbm.1, f32[512,256]{1,0:T(8,128)} %f_hbm.1, f32[512,256]{1,0:T(8,128)} %w_hbm.1), custom_call_target="tpu_custom_call" | custom-call | tf_op jit(solution)/shard_map/steps/pallas_call | solution.py:263
  49.0 0.0 copy-start.1
  49.0 1.9 %copy.11 = f32[512,256]{1,0:T(8,128)} copy(f32[512,256]{1,0:T(8,128)} %get-tuple-element.6) | data formatting | bytes 1048576
  50.9 0.0 copy-done.1
  50.9 0.0 copy-start
  50.9 0.8 %copy.12 = f32[512,256]{1,0:T(8,128)} copy(f32[512,256]{1,0:T(8,128)S(1)} %copy-done.1) | data formatting | bytes 1048576
  51.7 0.4 copy-done
  52.2 0.8 %copy.13 = f32[512,256]{1,0:T(8,128)} copy(f32[512,256]{1,0:T(8,128)S(1)} %copy-done) | data formatting | bytes 1048576
Async XLA Ops:
  49.0 1.9 %copy-start.1 = (f32[512,256]{1,0:T(8,128)S(1)}, f32[512,256]{1,0:T(8,128)}, u32[]{:S(2)}) copy-start(f32[512,256]{1,0:T(8,128)} %get-tuple-element.7) | copy-start | bytes 1572868
  50.9 1.2 %copy-start = (f32[512,256]{1,0:T(8,128)S(1)}, f32[512,256]{1,0:T(8,128)}, u32[]{:S(2)}) copy-start(f32[512,256]{1,0:T(8,128)} %get-tuple-element.8) | copy-start | bytes 1572868

commit v3 on v2

--- a/solution.py
+++ b/solution.py
@@ -27,9 +27,9 @@
     return [(part[b - 1, -1] + part[b, 0]) + part[b + 1, 1] for b in range(nb)]
 
 
-def kernel(row_size, col_size, core_size, tiles, wts_ref, gains_ref, u_hbm, f_hbm, w_hbm, uo_hbm, go_hbm, gf_hbm,
-           nat, ubase, lbase, inner, coef, force, acc, loc_sem, row_send, row_recv, f_send, f_recv,
-           u_send, u_recv, l_send, l_recv, out_sem):
+def kernel(row_size, col_size, core_size, tiles, wts_hbm, gains_hbm, u_hbm, f_hbm, w_hbm, uo_ref, go_ref, gf_ref,
+           wts_ref, gains_ref, nat, ubase, lbase, inner, coef, force, acc, par_sem, loc_sem, row_send, row_recv, f_send, f_recv,
+           u_send, u_recv, l_send, l_recv):
     rows, width, steps = tiles
     nb = force.shape[0]
     halo = (nb * LANES - rows) // 2
@@ -53,9 +53,13 @@
     cblocks = width // LANES
     local = [[pltpu.make_async_copy(srcs[k].at[:, pl.ds(cb * LANES, LANES)], nat.at[k, cb, pl.ds(halo, rows), :],
                                     loc_sem.at[k, cb]) for cb in range(cblocks)] for k in range(3)]
-    for k in range(2):
+    for k in range(3):
         for copy in local[k]:
             copy.start()
+    params = [pltpu.make_async_copy(wts_hbm, wts_ref, par_sem.at[0]),
+              pltpu.make_async_copy(gains_hbm, gains_ref, par_sem.at[1])]
+    for copy in params:
+        copy.start()
 
     barrier = pltpu.get_barrier_semaphore()
     for dev in (above, below, left, right):
@@ -66,12 +70,11 @@
         dep = halo if k < 2 else half
         out = []
         for cb in range(cblocks):
-            lanes = pl.ds(cb * LANES, LANES)
             out.append(pltpu.make_async_remote_copy(
-                srcs[k].at[pl.ds(0, dep), lanes], nat.at[k, cb, pl.ds(halo + rows, dep), :],
+                nat.at[k, cb, pl.ds(halo, dep), :], nat.at[k, cb, pl.ds(halo + rows, dep), :],
                 row_send.at[k, cb, 0], row_recv.at[k, cb, 0], device_id=above, device_id_type=MESH))
             out.append(pltpu.make_async_remote_copy(
-                srcs[k].at[pl.ds(rows - dep, dep), lanes], nat.at[k, cb, pl.ds(halo - dep, dep), :],
+                nat.at[k, cb, pl.ds(halo + rows - dep, dep), :], nat.at[k, cb, pl.ds(halo - dep, dep), :],
                 row_send.at[k, cb, 1], row_recv.at[k, cb, 1], device_id=below, device_id_type=MESH))
         return out
 
@@ -84,17 +87,15 @@
         ]
 
     rcopies = [row_copies(k) for k in range(3)]
-    for k in range(2):
+    for k in range(3):
+        for copy in local[k]:
+            copy.wait()
         for copy in rcopies[k]:
             copy.start()
-    for copy in local[2]:
-        copy.start()
-    for copy in rcopies[2]:
-        copy.start()
+    for copy in params:
+        copy.wait()
 
     def arrive(k, dst, factor):
-        for copy in local[k]:
-            copy.wait()
         for copy in rcopies[k]:
             copy.wait()
         for cb in range(cblocks):
@@ -111,8 +112,7 @@
                 if factor is not None:
                     val = val * factor
                 nat[k, cb, pl.ds(b, LANES, stride=nb), :] = val
-        return [pltpu.make_async_copy(nat.at[k, cb, pl.ds(halo, rows), :], out.at[:, pl.ds(cb * LANES, LANES)],
-                                      out_sem.at[k, cb]) for cb in range(cblocks)]
+            out[:, pl.ds(cb * LANES, LANES)] = nat[k, cb, pl.ds(halo, rows), :]
 
     arrive(0, ubase.at[0], scale)
     for copy in col_copies(ubase.at[0], fdep, u_send.at[0], u_recv.at[0]):
@@ -202,9 +202,7 @@
     arrive(2, lbase.at[0], None)
     for copy in col_copies(lbase.at[0], adep, l_send.at[0], l_recv.at[0]):
         copy.start()
-    ucopies = depart(ubase.at[phases % 2], 0, uo_hbm, 1.0 / scale)
-    for copy in ucopies:
-        copy.start()
+    depart(ubase.at[phases % 2], 0, uo_ref, 1.0 / scale)
     acc[...] = jnp.zeros_like(acc)
 
     def adj_phase(phase, _):
@@ -236,14 +234,8 @@
 
     lax.fori_loop(0, phases, adj_phase, 0)
 
-    gcopies = depart(lbase.at[phases % 2], 1, go_hbm, None)
-    for copy in gcopies:
-        copy.start()
-    fo_copies = depart(acc, 2, gf_hbm, None)
-    for copy in fo_copies:
-        copy.start()
-    for copy in ucopies + gcopies + fo_copies:
-        copy.wait()
+    depart(lbase.at[phases % 2], 1, go_ref, None)
+    depart(acc, 2, gf_ref, None)
 
 
 def solution(mesh):
@@ -259,13 +251,15 @@
         f32 = jnp.float32
         field = (nb, cols, LANES)
         dma = pltpu.SemaphoreType.DMA
-        hbm, smem = pl.BlockSpec(memory_space=pl.ANY), pl.BlockSpec(memory_space=pltpu.SMEM)
+        hbm, vmem = pl.BlockSpec(memory_space=pl.ANY), pl.BlockSpec(memory_space=pltpu.VMEM)
         return pl.pallas_call(
             functools.partial(kernel, row_size, col_size, core_size, (rows, width, steps)),
             out_shape=[jax.ShapeDtypeStruct((rows, width), f32)] * 3,
-            in_specs=[smem, smem, hbm, hbm, hbm],
-            out_specs=[hbm, hbm, hbm],
+            in_specs=[hbm] * 5,
+            out_specs=[vmem, vmem, vmem],
             scratch_shapes=[
+                pltpu.SMEM(weights.shape, f32),
+                pltpu.SMEM(gains.shape, f32),
                 pltpu.VMEM((3, cblocks, nb * LANES, LANES), f32),
                 pltpu.VMEM((2,) + field, f32),
                 pltpu.VMEM((2,) + field, f32),
@@ -273,6 +267,7 @@
                 pltpu.VMEM((steps,) + field, f32),
                 pltpu.VMEM(field, f32),
                 pltpu.VMEM(field, f32),
+                dma((2,)),
                 dma((3, cblocks)),
                 dma((3, cblocks, 2)),
                 dma((3, cblocks, 2)),
@@ -282,12 +277,11 @@
                 dma((2, 2)),
                 dma((2, 2)),
                 dma((2, 2)),
-                dma((3, cblocks)),
             ],
             compiler_params=pltpu.CompilerParams(
-                collective_id=0, has_side_effects=True, vmem_limit_bytes=60 * 1024 * 1024),
+                collective_id=0, has_side_effects=True, vmem_limit_bytes=48 * 1024 * 1024),
             name="steps",
-        )(weights, gains, u_init, forcing, loss_weight)
+        )(*(pltpu.with_memory_space_constraint(x, pltpu.HBM) for x in (weights, gains, u_init, forcing, loss_weight)))
 
     return jax.shard_map(local_run, mesh=mesh, in_specs=(field_spec, field_spec, field_spec, P(), P()),
                          out_specs=(field_spec, field_spec, field_spec), check_vma=False)

time: 53.6 us -> 51.3 us (0.957); the launches traced: 53 us -> 51.2 us
  local copies, waits for them, and re-layouts: 3.95 us -> 2.38 us
    unnamed x7 -> x3, local copies, waits for them, and re-layouts: 3.95 us -> 2.38 us
where the time goes in v3:
time: 51.3 us; the launch traced here: 51.2 us
  Pallas kernels  48.2 us (94%)
  local copies, waits for them, and re-layouts  2.38 us (5%)
  between operations  0.64 us (1%)
    pallas_call x1, Pallas kernels, local_run(): pl.pallas_call(functools.partial(kernel, row_size, col_size, core_size, (...  48.2 us
    unnamed x3, local copies, waits for them, and re-layouts  2.38 us

profile of v3, /device:TPU:97, one launch (start us, length us, event | category | flops | bytes accessed | tf_op | source)
XLA Modules:
  0.0 51.2 jit_solution(16681165877739258683)
XLA Ops:
  0.6 48.2 %steps.1 = (f32[512,256]{1,0:T(8,128)S(1)}, f32[512,256]{1,0:T(8,128)S(1)}, f32[512,256]{1,0:T(8,128)S(1)}) custom-call(f32[3,3]{1,0:T(4,128)} %wts_hbm.1, f32[32]{0:T(128)} %gains_hbm.1, f32[512,256]{1,0:T(8,128)} %u_hbm.1, f32[512,256]{1,0:T(8,128)} %f_hbm.1, f32[512,256]{1,0:T(8,128)} %w_hbm.1), custom_call_target="tpu_custom_call" | custom-call | tf_op jit(solution)/shard_map/steps/pallas_call | solution.py:255
  48.8 0.8 %copy.11 = f32[512,256]{1,0:T(8,128)} copy(f32[512,256]{1,0:T(8,128)S(1)} %get-tuple-element.6) | data formatting | bytes 1048576
  49.6 0.8 %copy.12 = f32[512,256]{1,0:T(8,128)} copy(f32[512,256]{1,0:T(8,128)S(1)} %get-tuple-element.7) | data formatting | bytes 1048576
  50.4 0.8 %copy.13 = f32[512,256]{1,0:T(8,128)} copy(f32[512,256]{1,0:T(8,128)S(1)} %get-tuple-element.8) | data formatting | bytes 1048576

commit v4 on v3

--- a/solution.py
+++ b/solution.py
@@ -11,6 +11,7 @@
 DT = 0.01
 LANES = 128
 PHASE = 8
+APART = 4
 UNROLL = 8
 MESH = pl.DeviceIdType.MESH
 
@@ -127,34 +128,26 @@
     mid_wt = wts_ref[1, 1] + DT
 
     def sweep(body, base, count):
-        full, rest = divmod(count, UNROLL)
-        if full == 1:
-            body(base, 8 * UNROLL)
-        elif full > 1:
-            def block(i, _):
-                body(base + i * (8 * UNROLL), 8 * UNROLL)
-                return 0
-            lax.fori_loop(0, full, block, 0)
-        if rest:
-            body(base + full * 8 * UNROLL, 8 * rest)
+        for off in range(0, count, 8 * UNROLL):
+            body(base + off, min(8 * UNROLL, count - off))
 
     def cover(step_body, dep):
         def middle():
             for j in range(1, PHASE + 1):
-                sweep(functools.partial(step_body, j), org + j, groups - j)
+                sweep(functools.partial(step_body, j), org + j, width - 2 * j)
 
         def sides():
             for j in range(1, PHASE):
-                sweep(functools.partial(step_body, j), org + j - dep, dep // 8)
-                sweep(functools.partial(step_body, j), org + width - 7 * j, -(-(dep + 6 * j) // 8))
-            sweep(functools.partial(step_body, PHASE), org, PHASE // 8)
-            sweep(functools.partial(step_body, PHASE), org + width - 7 * PHASE, 7 * PHASE // 8)
+                sweep(functools.partial(step_body, j), org + j - dep, dep)
+                sweep(functools.partial(step_body, j), org + width - j, dep)
+            sweep(functools.partial(step_body, PHASE), org, PHASE)
+            sweep(functools.partial(step_body, PHASE), org + width - PHASE, PHASE)
         return middle, sides
 
     def level(base, par, j):
         if j == 0:
-            return base.at[par]
-        return base.at[1 - par] if j == PHASE else inner.at[j - 1]
+            return base.at[par * APART]
+        return base.at[(1 - par) * APART] if j == PHASE else inner.at[j - 1]
 
     def reaction(val, t, b, at):
         sq = val * val
@@ -178,7 +171,7 @@
 
         middle, sides = cover(step_body, fdep)
         middle()
-        for copy in col_copies(ubase.at[par], fdep, u_send.at[par], u_recv.at[par]):
+        for copy in col_copies(ubase.at[par * APART], fdep, u_send.at[par], u_recv.at[par]):
             copy.wait()
 
         @pl.when(phase == 0)
@@ -193,7 +186,7 @@
 
         @pl.when(phase < phases - 1)
         def _():
-            for copy in col_copies(ubase.at[1 - par], fdep, u_send.at[1 - par], u_recv.at[1 - par]):
+            for copy in col_copies(ubase.at[(1 - par) * APART], fdep, u_send.at[1 - par], u_recv.at[1 - par]):
                 copy.start()
         return 0
 
@@ -202,7 +195,7 @@
     arrive(2, lbase.at[0], None)
     for copy in col_copies(lbase.at[0], adep, l_send.at[0], l_recv.at[0]):
         copy.start()
-    depart(ubase.at[phases % 2], 0, uo_ref, 1.0 / scale)
+    depart(ubase.at[phases % 2 * APART], 0, uo_ref, 1.0 / scale)
     acc[...] = jnp.zeros_like(acc)
 
     def adj_phase(phase, _):
@@ -222,19 +215,19 @@
 
         middle, sides = cover(step_body, adep)
         middle()
-        for copy in col_copies(lbase.at[par], adep, l_send.at[par], l_recv.at[par]):
+        for copy in col_copies(lbase.at[par * APART], adep, l_send.at[par], l_recv.at[par]):
             copy.wait()
         sides()
 
         @pl.when(phase < phases - 1)
         def _():
-            for copy in col_copies(lbase.at[1 - par], adep, l_send.at[1 - par], l_recv.at[1 - par]):
+            for copy in col_copies(lbase.at[(1 - par) * APART], adep, l_send.at[1 - par], l_recv.at[1 - par]):
                 copy.start()
         return 0
 
     lax.fori_loop(0, phases, adj_phase, 0)
 
-    depart(lbase.at[phases % 2], 1, go_ref, None)
+    depart(lbase.at[phases % 2 * APART], 1, go_ref, None)
     depart(acc, 2, gf_ref, None)
 
 
@@ -261,8 +254,8 @@
                 pltpu.SMEM(weights.shape, f32),
                 pltpu.SMEM(gains.shape, f32),
                 pltpu.VMEM((3, cblocks, nb * LANES, LANES), f32),
-                pltpu.VMEM((2,) + field, f32),
-                pltpu.VMEM((2,) + field, f32),
+                pltpu.VMEM((1 + APART,) + field, f32),
+                pltpu.VMEM((1 + APART,) + field, f32),
                 pltpu.VMEM((PHASE - 1,) + field, f32),
                 pltpu.VMEM((steps,) + field, f32),
                 pltpu.VMEM(field, f32),

time: 51.3 us -> 49.8 us (0.971)
  Pallas kernels: 48.2 us -> 46.7 us
    pallas_call x1, Pallas kernels: 48.2 us -> 46.7 us  [local_run(): pl.pallas_call(functools.partial(kernel, row_size, col_size, core_size, (...]
where the time goes in v4:
time: 49.8 us; the launch traced here: 49.7 us
  Pallas kernels  46.7 us (94%)
  local copies, waits for them, and re-layouts  2.38 us (5%)
  between operations  0.64 us (1%)
    pallas_call x1, Pallas kernels, local_run(): pl.pallas_call(functools.partial(kernel, row_size, col_size, core_size, (...  46.7 us
    unnamed x3, local copies, waits for them, and re-layouts  2.38 us

profile of v4, /device:TPU:97, one launch (start us, length us, event | category | flops | bytes accessed | tf_op | source)
XLA Modules:
  0.0 49.7 jit_solution(15785034116004910661)
XLA Ops:
  0.6 46.7 %steps.1 = (f32[512,256]{1,0:T(8,128)S(1)}, f32[512,256]{1,0:T(8,128)S(1)}, f32[512,256]{1,0:T(8,128)S(1)}) custom-call(f32[3,3]{1,0:T(4,128)} %wts_hbm.1, f32[32]{0:T(128)} %gains_hbm.1, f32[512,256]{1,0:T(8,128)} %u_hbm.1, f32[512,256]{1,0:T(8,128)} %f_hbm.1, f32[512,256]{1,0:T(8,128)} %w_hbm.1), custom_call_target="tpu_custom_call" | custom-call | tf_op jit(solution)/shard_map/steps/pallas_call | solution.py:248
  47.3 0.8 %copy.11 = f32[512,256]{1,0:T(8,128)} copy(f32[512,256]{1,0:T(8,128)S(1)} %get-tuple-element.6) | data formatting | bytes 1048576
  48.1 0.8 %copy.12 = f32[512,256]{1,0:T(8,128)} copy(f32[512,256]{1,0:T(8,128)S(1)} %get-tuple-element.7) | data formatting | bytes 1048576
  48.9 0.8 %copy.13 = f32[512,256]{1,0:T(8,128)} copy(f32[512,256]{1,0:T(8,128)S(1)} %get-tuple-element.8) | data formatting | bytes 1048576

commit v5 on v4

--- a/solution.py
+++ b/solution.py
@@ -11,7 +11,7 @@
 DT = 0.01
 LANES = 128
 PHASE = 8
-APART = 4
+BANKED = 4
 UNROLL = 8
 MESH = pl.DeviceIdType.MESH
 
@@ -28,10 +28,11 @@
     return [(part[b - 1, -1] + part[b, 0]) + part[b + 1, 1] for b in range(nb)]
 
 
-def kernel(row_size, col_size, core_size, tiles, wts_hbm, gains_hbm, u_hbm, f_hbm, w_hbm, uo_ref, go_ref, gf_ref,
-           wts_ref, gains_ref, nat, ubase, lbase, inner, coef, force, acc, par_sem, loc_sem, row_send, row_recv, f_send, f_recv,
+def kernel(row_size, col_size, core_size, tiles, wts_hbm, gains_hbm, u_hbm, f_hbm, w_hbm, uo_ref, lo_ref, ao_ref,
+           wts_ref, gains_ref, nat, ubase, lbase, inner, coef, forces, par_sem, loc_sem, row_send, row_recv, f_send, f_recv,
            u_send, u_recv, l_send, l_recv):
     rows, width, steps = tiles
+    force = acc = forces.at[0]
     nb = force.shape[0]
     halo = (nb * LANES - rows) // 2
     half = halo // 2
@@ -146,8 +147,8 @@
 
     def level(base, par, j):
         if j == 0:
-            return base.at[par * APART]
-        return base.at[(1 - par) * APART] if j == PHASE else inner.at[j - 1]
+            return base.at[par * BANKED]
+        return base.at[(1 - par) * BANKED] if j == PHASE else inner.at[j - 1]
 
     def reaction(val, t, b, at):
         sq = val * val
@@ -171,7 +172,7 @@
 
         middle, sides = cover(step_body, fdep)
         middle()
-        for copy in col_copies(ubase.at[par * APART], fdep, u_send.at[par], u_recv.at[par]):
+        for copy in col_copies(ubase.at[par * BANKED], fdep, u_send.at[par], u_recv.at[par]):
             copy.wait()
 
         @pl.when(phase == 0)
@@ -186,7 +187,7 @@
 
         @pl.when(phase < phases - 1)
         def _():
-            for copy in col_copies(ubase.at[(1 - par) * APART], fdep, u_send.at[1 - par], u_recv.at[1 - par]):
+            for copy in col_copies(ubase.at[(1 - par) * BANKED], fdep, u_send.at[1 - par], u_recv.at[1 - par]):
                 copy.start()
         return 0
 
@@ -195,8 +196,8 @@
     arrive(2, lbase.at[0], None)
     for copy in col_copies(lbase.at[0], adep, l_send.at[0], l_recv.at[0]):
         copy.start()
-    depart(ubase.at[phases % 2 * APART], 0, uo_ref, 1.0 / scale)
-    acc[...] = jnp.zeros_like(acc)
+    depart(ubase.at[phases % 2 * BANKED], 0, uo_ref, 1.0 / scale)
+    acc[...] = jnp.zeros(acc.shape, jnp.float32)
 
     def adj_phase(phase, _):
         par = lax.rem(phase, 2)
@@ -215,20 +216,37 @@
 
         middle, sides = cover(step_body, adep)
         middle()
-        for copy in col_copies(lbase.at[par * APART], adep, l_send.at[par], l_recv.at[par]):
+        for copy in col_copies(lbase.at[par * BANKED], adep, l_send.at[par], l_recv.at[par]):
             copy.wait()
         sides()
 
         @pl.when(phase < phases - 1)
         def _():
-            for copy in col_copies(lbase.at[(1 - par) * APART], adep, l_send.at[1 - par], l_recv.at[1 - par]):
+            for copy in col_copies(lbase.at[(1 - par) * BANKED], adep, l_send.at[1 - par], l_recv.at[1 - par]):
                 copy.start()
         return 0
 
     lax.fori_loop(0, phases, adj_phase, 0)
 
-    depart(lbase.at[phases % 2 * APART], 1, go_ref, None)
-    depart(acc, 2, gf_ref, None)
+    lo_ref[...] = lbase[phases % 2 * BANKED, :, pl.ds(org, width), :]
+    ao_ref[...] = acc[:, pl.ds(org, width), :]
+
+
+def unlane(tiles, u_ref, l_ref, a_ref, uo_hbm, go_hbm, gf_hbm, nat, sem):
+    rows, width = tiles
+    nb = l_ref.shape[0]
+    halo = (nb * LANES - rows) // 2
+    copies = [pltpu.make_async_copy(u_ref, uo_hbm, sem.at[0, 0])]
+    copies[0].start()
+    for k, (src, out) in enumerate(((l_ref, go_hbm), (a_ref, gf_hbm))):
+        for cb in range(width // LANES):
+            for b in range(nb):
+                nat[k, cb, pl.ds(b, LANES, stride=nb), :] = jnp.transpose(src[b, pl.ds(cb * LANES, LANES), :])
+            copies.append(pltpu.make_async_copy(nat.at[k, cb, pl.ds(halo, rows), :],
+                                                out.at[:, pl.ds(cb * LANES, LANES)], sem.at[k + 1, cb]))
+            copies[-1].start()
+    for copy in copies:
+        copy.wait()
 
 
 def solution(mesh):
@@ -245,21 +263,20 @@
         field = (nb, cols, LANES)
         dma = pltpu.SemaphoreType.DMA
         hbm, vmem = pl.BlockSpec(memory_space=pl.ANY), pl.BlockSpec(memory_space=pltpu.VMEM)
-        return pl.pallas_call(
+        lanes_out = pl.pallas_call(
             functools.partial(kernel, row_size, col_size, core_size, (rows, width, steps)),
-            out_shape=[jax.ShapeDtypeStruct((rows, width), f32)] * 3,
+            out_shape=[jax.ShapeDtypeStruct(dims, f32) for dims in ((rows, width), (nb, width, LANES), (nb, width, LANES))],
             in_specs=[hbm] * 5,
             out_specs=[vmem, vmem, vmem],
             scratch_shapes=[
                 pltpu.SMEM(weights.shape, f32),
                 pltpu.SMEM(gains.shape, f32),
                 pltpu.VMEM((3, cblocks, nb * LANES, LANES), f32),
-                pltpu.VMEM((1 + APART,) + field, f32),
-                pltpu.VMEM((1 + APART,) + field, f32),
-                pltpu.VMEM((PHASE - 1,) + field, f32),
+                pltpu.VMEM((2 * BANKED,) + field, f32),
+                pltpu.VMEM((2 * BANKED,) + field, f32),
+                pltpu.VMEM((PHASE,) + field, f32),
                 pltpu.VMEM((steps,) + field, f32),
-                pltpu.VMEM(field, f32),
-                pltpu.VMEM(field, f32),
+                pltpu.VMEM((BANKED,) + field, f32),
                 dma((2,)),
                 dma((3, cblocks)),
                 dma((3, cblocks, 2)),
@@ -272,9 +289,18 @@
                 dma((2, 2)),
             ],
             compiler_params=pltpu.CompilerParams(
-                collective_id=0, has_side_effects=True, vmem_limit_bytes=48 * 1024 * 1024),
+                collective_id=0, has_side_effects=True, vmem_limit_bytes=52 * 1024 * 1024),
             name="steps",
         )(*(pltpu.with_memory_space_constraint(x, pltpu.HBM) for x in (weights, gains, u_init, forcing, loss_weight)))
+        return pl.pallas_call(
+            functools.partial(unlane, (rows, width)),
+            out_shape=[jax.ShapeDtypeStruct((rows, width), f32)] * 3,
+            in_specs=[vmem] * 3,
+            out_specs=[hbm] * 3,
+            scratch_shapes=[pltpu.VMEM((2, cblocks, nb * LANES, LANES), f32), dma((3, 2))],
+            compiler_params=pltpu.CompilerParams(vmem_limit_bytes=16 * 1024 * 1024),
+            name="unlane",
+        )(*(pltpu.with_memory_space_constraint(x, pltpu.VMEM) for x in lanes_out))
 
     return jax.shard_map(local_run, mesh=mesh, in_specs=(field_spec, field_spec, field_spec, P(), P()),
                          out_specs=(field_spec, field_spec, field_spec), check_vma=False)

time: 49.8 us -> 48.4 us (0.972)
  local copies, waits for them, and re-layouts: 2.38 us -> 0 us
  Pallas kernels: 46.7 us -> 47.6 us
    unnamed x3 -> x0, local copies, waits for them, and re-layouts: 2.38 us -> none
    pallas_call x0 -> x1, Pallas kernels: none -> 1.19 us  [local_run(): pl.pallas_call(functools.partial(unlane, (rows, width)), out_shape=[jax.S...]
where the time goes in v5:
time: 48.4 us; the launch traced here: 48.3 us
  Pallas kernels  47.6 us (98%)
  between operations  0.64 us (1%)
    pallas_call x1, Pallas kernels, local_run(): pl.pallas_call(functools.partial(kernel, row_size, col_size, core_size, (...  46.4 us
    pallas_call x1, Pallas kernels, local_run(): pl.pallas_call(functools.partial(unlane, (rows, width)), out_shape=[jax.S...  1.19 us

profile of v5, /device:TPU:97, one launch (start us, length us, event | category | flops | bytes accessed | tf_op | source)
XLA Modules:
  0.0 48.3 jit_solution(5024337450198031030)
XLA Ops:
  0.6 46.4 %steps.1 = (f32[512,256]{1,0:T(8,128)S(1)}, f32[5,256,128]{2,1,0:T(8,128)S(1)}, f32[5,256,128]{2,1,0:T(8,128)S(1)}) custom-call(f32[3,3]{1,0:T(4,128)} %wts_hbm.1, f32[32]{0:T(128)} %gains_hbm.1, f32[512,256]{1,0:T(8,128)} %u_hbm.1, f32[512,256]{1,0:T(8,128)} %f_hbm.1, f32[512,256]{1,0:T(8,128)} %w_hbm.1), custom_call_target="tpu_custom_call" | custom-call | tf_op jit(solution)/shard_map/steps/pallas_call | solution.py:266
  47.1 1.2 %unlane.1 = (f32[512,256]{1,0:T(8,128)}, f32[512,256]{1,0:T(8,128)}, f32[512,256]{1,0:T(8,128)}) custom-call(f32[512,256]{1,0:T(8,128)S(1)} %get-tuple-element.6.u_ref, f32[5,256,128]{2,1,0:T(8,128)S(1)} %get-tuple-element.7.l_ref, f32[5,256,128]{2,1,0:T(8,128)S(1)} %get-tuple-element.8.a_ref), custom_call_target="tpu_custom_call" | custom-call | tf_op jit(solution)/shard_map/unlane/pallas_call | solution.py:295

commit v6 on v5

--- a/solution.py
+++ b/solution.py
@@ -70,15 +70,13 @@
 
     def row_copies(k):
         dep = halo if k < 2 else half
-        out = []
-        for cb in range(cblocks):
-            out.append(pltpu.make_async_remote_copy(
-                nat.at[k, cb, pl.ds(halo, dep), :], nat.at[k, cb, pl.ds(halo + rows, dep), :],
-                row_send.at[k, cb, 0], row_recv.at[k, cb, 0], device_id=above, device_id_type=MESH))
-            out.append(pltpu.make_async_remote_copy(
-                nat.at[k, cb, pl.ds(halo + rows - dep, dep), :], nat.at[k, cb, pl.ds(halo - dep, dep), :],
-                row_send.at[k, cb, 1], row_recv.at[k, cb, 1], device_id=below, device_id_type=MESH))
-        return out
+        strip = lambda first: nat.at[k, :, pl.ds(first, dep), :]
+        return [
+            pltpu.make_async_remote_copy(strip(halo), strip(halo + rows), row_send.at[k, 0], row_recv.at[k, 0],
+                                         device_id=above, device_id_type=MESH),
+            pltpu.make_async_remote_copy(strip(halo + rows - dep), strip(halo - dep), row_send.at[k, 1],
+                                         row_recv.at[k, 1], device_id=below, device_id_type=MESH),
+        ]
 
     def col_copies(ref, dep, send, recv):
         return [
@@ -119,11 +117,6 @@
     arrive(0, ubase.at[0], scale)
     for copy in col_copies(ubase.at[0], fdep, u_send.at[0], u_recv.at[0]):
         copy.start()
-    arrive(1, force, scale)
-    fcopies = col_copies(force, fdep, f_send, f_recv)
-    for copy in fcopies:
-        copy.start()
-
     wts = [[wts_ref[i, j] for j in range(3)] for i in range(3)]
     flip = [[wts_ref[2 - i, 2 - j] for j in range(3)] for i in range(3)]
     mid_wt = wts_ref[1, 1] + DT
@@ -133,8 +126,11 @@
             body(base + off, min(8 * UNROLL, count - off))
 
     def cover(step_body, dep):
+        def first():
+            sweep(functools.partial(step_body, 1), org + 1, width - 2)
+
         def middle():
-            for j in range(1, PHASE + 1):
+            for j in range(2, PHASE + 1):
                 sweep(functools.partial(step_body, j), org + j, width - 2 * j)
 
         def sides():
@@ -143,7 +139,7 @@
                 sweep(functools.partial(step_body, j), org + width - j, dep)
             sweep(functools.partial(step_body, PHASE), org, PHASE)
             sweep(functools.partial(step_body, PHASE), org + width - PHASE, PHASE)
-        return middle, sides
+        return first, middle, sides
 
     def level(base, par, j):
         if j == 0:
@@ -156,21 +152,30 @@
         coef[t, b, at, :] = (weight - sq) - sq
         return weight
 
+    def fwd_body(phase, forced, j, base, cols):
+        par = lax.rem(phase, 2)
+        src, dst, t = level(ubase, par, j - 1), level(ubase, par, j), phase * PHASE + (j - 1)
+        at = pl.ds(base, cols)
+        sums = stencil_blocks(lambda b, d: src[b, pl.ds(base + d, cols), :], wts,
+                              lambda b, mid: reaction(mid, t, b, at), nb)
+        for b in range(nb):
+            dst[b, at, :] = sums[b] + gains_ref[t] * force[b, at, :] if forced else sums[b]
+
+    sweep(functools.partial(fwd_body, 0, False, 1), org + 1, width - 2)
+    arrive(1, force, scale)
+    fcopies = col_copies(force, fdep, f_send, f_recv)
+    for copy in fcopies:
+        copy.start()
+
+    for b in range(nb):
+        at = pl.ds(org + 1, width - 2)
+        inner[0, b, at, :] = inner[0, b, at, :] + gains_ref[0] * force[b, at, :]
+
     def fwd_phase(phase, _):
         par = lax.rem(phase, 2)
-
-        def step_body(j, base, cols):
-            src, dst, t = level(ubase, par, j - 1), level(ubase, par, j), phase * PHASE + (j - 1)
-            gain = gains_ref[t]
-            at = pl.ds(base, cols)
-
-            def centre(b, mid):
-                return reaction(mid, t, b, at)
-            sums = stencil_blocks(lambda b, d: src[b, pl.ds(base + d, cols), :], wts, centre, nb)
-            for b in range(nb):
-                dst[b, at, :] = sums[b] + gain * force[b, at, :]
-
-        middle, sides = cover(step_body, fdep)
+        step_body = functools.partial(fwd_body, phase, True)
+        first, middle, sides = cover(step_body, fdep)
+        pl.when(phase > 0)(first)
         middle()
         for copy in col_copies(ubase.at[par * BANKED], fdep, u_send.at[par], u_recv.at[par]):
             copy.wait()
@@ -214,7 +219,8 @@
             for b in range(nb):
                 dst[b, at, :] = sums[b]
 
-        middle, sides = cover(step_body, adep)
+        first, middle, sides = cover(step_body, adep)
+        first()
         middle()
         for copy in col_copies(lbase.at[par * BANKED], adep, l_send.at[par], l_recv.at[par]):
             copy.wait()
@@ -279,8 +285,8 @@
                 pltpu.VMEM((BANKED,) + field, f32),
                 dma((2,)),
                 dma((3, cblocks)),
-                dma((3, cblocks, 2)),
-                dma((3, cblocks, 2)),
+                dma((3, 2)),
+                dma((3, 2)),
                 dma((2,)),
                 dma((2,)),
                 dma((2, 2)),

time: 48.4 us -> 48.1 us (level)
  no operation moved by 1% of the time
where the time goes in v6:
time: 48.1 us; the launch traced here: 48 us
  Pallas kernels  47.3 us (98%)
  between operations  0.64 us (1%)
    pallas_call x1, Pallas kernels, local_run(): pl.pallas_call(functools.partial(kernel, row_size, col_size, core_size, (...  46.2 us
    pallas_call x1, Pallas kernels, local_run(): pl.pallas_call(functools.partial(unlane, (rows, width)), out_shape=[jax.S...  1.19 us

profile of v6, /device:TPU:97, one launch (start us, length us, event | category | flops | bytes accessed | tf_op | source)
XLA Modules:
  0.0 48.0 jit_solution(13415523691766906732)
XLA Ops:
  0.6 46.2 %steps.1 = (f32[512,256]{1,0:T(8,128)S(1)}, f32[5,256,128]{2,1,0:T(8,128)S(1)}, f32[5,256,128]{2,1,0:T(8,128)S(1)}) custom-call(f32[3,3]{1,0:T(4,128)} %wts_hbm.1, f32[32]{0:T(128)} %gains_hbm.1, f32[512,256]{1,0:T(8,128)} %u_hbm.1, f32[512,256]{1,0:T(8,128)} %f_hbm.1, f32[512,256]{1,0:T(8,128)} %w_hbm.1), custom_call_target="tpu_custom_call" | custom-call | tf_op jit(solution)/shard_map/steps/pallas_call | solution.py:272
  46.8 1.2 %unlane.1 = (f32[512,256]{1,0:T(8,128)}, f32[512,256]{1,0:T(8,128)}, f32[512,256]{1,0:T(8,128)}) custom-call(f32[512,256]{1,0:T(8,128)S(1)} %get-tuple-element.6.u_ref, f32[5,256,128]{2,1,0:T(8,128)S(1)} %get-tuple-element.7.l_ref, f32[5,256,128]{2,1,0:T(8,128)S(1)} %get-tuple-element.8.a_ref), custom_call_target="tpu_custom_call" | custom-call | tf_op jit(solution)/shard_map/unlane/pallas_call | solution.py:301

commit v7 on v6

--- a/solution.py
+++ b/solution.py
@@ -32,7 +32,7 @@
            wts_ref, gains_ref, nat, ubase, lbase, inner, coef, forces, par_sem, loc_sem, row_send, row_recv, f_send, f_recv,
            u_send, u_recv, l_send, l_recv):
     rows, width, steps = tiles
-    force = acc = forces.at[0]
+    force, acc = forces.at[0], ao_ref
     nb = force.shape[0]
     halo = (nb * LANES - rows) // 2
     half = halo // 2
@@ -51,21 +51,32 @@
     left = {"col": lax.div(lflat, core_size), "core": lax.rem(lflat, core_size)}
     right = {"col": lax.div(rflat, core_size), "core": lax.rem(rflat, core_size)}
 
+    barrier = pltpu.get_barrier_semaphore()
+    for dev in (above, below, left, right):
+        pl.semaphore_signal(barrier, inc=1, device_id=dev, device_id_type=MESH)
+
     srcs = (u_hbm, f_hbm, w_hbm)
     cblocks = width // LANES
-    local = [[pltpu.make_async_copy(srcs[k].at[:, pl.ds(cb * LANES, LANES)], nat.at[k, cb, pl.ds(halo, rows), :],
-                                    loc_sem.at[k, cb]) for cb in range(cblocks)] for k in range(3)]
-    for k in range(3):
-        for copy in local[k]:
-            copy.start()
+
+    def fetch(k):
+        dep = halo if k < 2 else half
+
+        def part(n, first, count):
+            return [pltpu.make_async_copy(
+                srcs[k].at[pl.ds(first, count), pl.ds(cb * LANES, LANES)],
+                nat.at[k, cb, pl.ds(halo + first, count), :], loc_sem.at[k, cb, n]) for cb in range(cblocks)]
+        return part(0, 0, dep) + part(1, rows - dep, dep), part(2, dep, rows - 2 * dep)
+
+    local = [fetch(k) for k in range(3)]
+    for copy in local[0][0] + local[0][1]:
+        copy.start()
     params = [pltpu.make_async_copy(wts_hbm, wts_ref, par_sem.at[0]),
               pltpu.make_async_copy(gains_hbm, gains_ref, par_sem.at[1])]
     for copy in params:
         copy.start()
-
-    barrier = pltpu.get_barrier_semaphore()
-    for dev in (above, below, left, right):
-        pl.semaphore_signal(barrier, inc=1, device_id=dev, device_id_type=MESH)
+    for k in (1, 2):
+        for copy in local[k][0] + local[k][1]:
+            copy.start()
     pl.semaphore_wait(barrier, 4)
 
     def row_copies(k):
@@ -88,7 +99,7 @@
 
     rcopies = [row_copies(k) for k in range(3)]
     for k in range(3):
-        for copy in local[k]:
+        for copy in local[k][0]:
             copy.wait()
         for copy in rcopies[k]:
             copy.start()
@@ -96,7 +107,7 @@
         copy.wait()
 
     def arrive(k, dst, factor):
-        for copy in rcopies[k]:
+        for copy in local[k][1] + rcopies[k]:
             copy.wait()
         for cb in range(cblocks):
             for b in range(nb):
@@ -235,19 +246,18 @@
     lax.fori_loop(0, phases, adj_phase, 0)
 
     lo_ref[...] = lbase[phases % 2 * BANKED, :, pl.ds(org, width), :]
-    ao_ref[...] = acc[:, pl.ds(org, width), :]
-
-
-def unlane(tiles, u_ref, l_ref, a_ref, uo_hbm, go_hbm, gf_hbm, nat, sem):
+
+
+def unlane(tiles, org, u_ref, l_ref, a_ref, uo_hbm, go_hbm, gf_hbm, nat, sem):
     rows, width = tiles
     nb = l_ref.shape[0]
     halo = (nb * LANES - rows) // 2
     copies = [pltpu.make_async_copy(u_ref, uo_hbm, sem.at[0, 0])]
     copies[0].start()
-    for k, (src, out) in enumerate(((l_ref, go_hbm), (a_ref, gf_hbm))):
+    for k, (src, first, out) in enumerate(((l_ref, 0, go_hbm), (a_ref, org, gf_hbm))):
         for cb in range(width // LANES):
             for b in range(nb):
-                nat[k, cb, pl.ds(b, LANES, stride=nb), :] = jnp.transpose(src[b, pl.ds(cb * LANES, LANES), :])
+                nat[k, cb, pl.ds(b, LANES, stride=nb), :] = jnp.transpose(src[b, pl.ds(first + cb * LANES, LANES), :])
             copies.append(pltpu.make_async_copy(nat.at[k, cb, pl.ds(halo, rows), :],
                                                 out.at[:, pl.ds(cb * LANES, LANES)], sem.at[k + 1, cb]))
             copies[-1].start()
@@ -271,7 +281,7 @@
         hbm, vmem = pl.BlockSpec(memory_space=pl.ANY), pl.BlockSpec(memory_space=pltpu.VMEM)
         lanes_out = pl.pallas_call(
             functools.partial(kernel, row_size, col_size, core_size, (rows, width, steps)),
-            out_shape=[jax.ShapeDtypeStruct(dims, f32) for dims in ((rows, width), (nb, width, LANES), (nb, width, LANES))],
+            out_shape=[jax.ShapeDtypeStruct(dims, f32) for dims in ((rows, width), (nb, width, LANES), field)],
             in_specs=[hbm] * 5,
             out_specs=[vmem, vmem, vmem],
             scratch_shapes=[
@@ -284,7 +294,7 @@
                 pltpu.VMEM((steps,) + field, f32),
                 pltpu.VMEM((BANKED,) + field, f32),
                 dma((2,)),
-                dma((3, cblocks)),
+                dma((3, cblocks, 3)),
                 dma((3, 2)),
                 dma((3, 2)),
                 dma((2,)),
@@ -299,7 +309,7 @@
             name="steps",
         )(*(pltpu.with_memory_space_constraint(x, pltpu.HBM) for x in (weights, gains, u_init, forcing, loss_weight)))
         return pl.pallas_call(
-            functools.partial(unlane, (rows, width)),
+            functools.partial(unlane, (rows, width), 2 * PHASE),
             out_shape=[jax.ShapeDtypeStruct((rows, width), f32)] * 3,
             in_specs=[vmem] * 3,
             out_specs=[hbm] * 3,

time: 48.1 us -> 48 us (level)
  no operation moved by 1% of the time
where the time goes in v7:
time: 48 us; the launch traced here: 47.9 us
  Pallas kernels  47.3 us (99%)
  between operations  0.64 us (1%)
    pallas_call x1, Pallas kernels, local_run(): pl.pallas_call(functools.partial(kernel, row_size, col_size, core_size, (...  46.1 us
    pallas_call x1, Pallas kernels, local_run(): pl.pallas_call(functools.partial(unlane, (rows, width), 2 * PHASE), out_s...  1.19 us

profile of v7, /device:TPU:97, one launch (start us, length us, event | category | flops | bytes accessed | tf_op | source)
XLA Modules:
  0.0 47.9 jit_solution(9431206460180858806)
XLA Ops:
  0.6 46.1 %steps.1 = (f32[512,256]{1,0:T(8,128)S(1)}, f32[5,256,128]{2,1,0:T(8,128)S(1)}, f32[5,296,128]{2,1,0:T(8,128)S(1)}) custom-call(f32[3,3]{1,0:T(4,128)} %wts_hbm.1, f32[32]{0:T(128)} %gains_hbm.1, f32[512,256]{1,0:T(8,128)} %u_hbm.1, f32[512,256]{1,0:T(8,128)} %f_hbm.1, f32[512,256]{1,0:T(8,128)} %w_hbm.1), custom_call_target="tpu_custom_call" | custom-call | tf_op jit(solution)/shard_map/steps/pallas_call | solution.py:282
  46.7 1.2 %unlane.1 = (f32[512,256]{1,0:T(8,128)}, f32[512,256]{1,0:T(8,128)}, f32[512,256]{1,0:T(8,128)}) custom-call(f32[512,256]{1,0:T(8,128)S(1)} %get-tuple-element.6.u_ref, f32[5,256,128]{2,1,0:T(8,128)S(1)} %get-tuple-element.7.l_ref, f32[5,296,128]{2,1,0:T(8,128)S(1)} %get-tuple-element.8.a_ref), custom_call_target="tpu_custom_call" | custom-call | tf_op jit(solution)/shard_map/unlane/pallas_call | solution.py:311

commit v8 on v7

--- a/solution.py
+++ b/solution.py
@@ -12,7 +12,7 @@
 LANES = 128
 PHASE = 8
 BANKED = 4
-UNROLL = 8
+UNROLL = 32
 MESH = pl.DeviceIdType.MESH
 
 
@@ -136,9 +136,15 @@
         for off in range(0, count, 8 * UNROLL):
             body(base + off, min(8 * UNROLL, count - off))
 
-    def cover(step_body, dep):
+    def cover(step_body, dep, ahead):
+        mark = width // 4 + 1
+
+        def early():
+            sweep(functools.partial(step_body, 1), org + mark, ahead)
+
         def first():
-            sweep(functools.partial(step_body, 1), org + 1, width - 2)
+            sweep(functools.partial(step_body, 1), org + 1, mark - 1)
+            sweep(functools.partial(step_body, 1), org + mark + ahead, width - 1 - mark - ahead)
 
         def middle():
             for j in range(2, PHASE + 1):
@@ -150,7 +156,7 @@
                 sweep(functools.partial(step_body, j), org + width - j, dep)
             sweep(functools.partial(step_body, PHASE), org, PHASE)
             sweep(functools.partial(step_body, PHASE), org + width - PHASE, PHASE)
-        return first, middle, sides
+        return early, first, middle, sides
 
     def level(base, par, j):
         if j == 0:
@@ -164,7 +170,7 @@
         return weight
 
     def fwd_body(phase, forced, j, base, cols):
-        par = lax.rem(phase, 2)
+        par = phase % 2 if isinstance(phase, int) else lax.rem(phase, 2)
         src, dst, t = level(ubase, par, j - 1), level(ubase, par, j), phase * PHASE + (j - 1)
         at = pl.ds(base, cols)
         sums = stencil_blocks(lambda b, d: src[b, pl.ds(base + d, cols), :], wts,
@@ -182,69 +188,88 @@
         at = pl.ds(org + 1, width - 2)
         inner[0, b, at, :] = inner[0, b, at, :] + gains_ref[0] * force[b, at, :]
 
-    def fwd_phase(phase, _):
-        par = lax.rem(phase, 2)
-        step_body = functools.partial(fwd_body, phase, True)
-        first, middle, sides = cover(step_body, fdep)
-        pl.when(phase > 0)(first)
+    def adj_body(phase, j, base, cols):
+        par = phase % 2 if isinstance(phase, int) else lax.rem(phase, 2)
+        src, dst, t = level(lbase, par, j - 1), level(lbase, par, j), steps - (phase * PHASE + j)
+        gain = gains_ref[t]
+        at = pl.ds(base, cols)
+
+        def centre(b, mid):
+            acc[b, at, :] += gain * mid
+            return coef[t, b, at, :]
+        sums = stencil_blocks(lambda b, d: src[b, pl.ds(base + d, cols), :], flip, centre, nb)
+        for b in range(nb):
+            dst[b, at, :] = sums[b]
+
+    def adj_sweeps(phase):
+        return cover(functools.partial(adj_body, phase), adep, width // 2)
+
+    def l_strips(phase):
+        par = phase % 2 if isinstance(phase, int) else lax.rem(phase, 2)
+        return col_copies(lbase.at[par * BANKED], adep, l_send.at[par], l_recv.at[par])
+
+    def adj_turn(phase, _):
+        for copy in l_strips(phase):
+            copy.wait()
+        early, first, middle, _ = adj_sweeps(phase + 1)
+        early()
+        adj_sweeps(phase)[3]()
+        for copy in l_strips(phase + 1):
+            copy.start()
+        first()
         middle()
-        for copy in col_copies(ubase.at[par * BANKED], fdep, u_send.at[par], u_recv.at[par]):
+        return 0
+
+    def fwd_sweeps(phase):
+        return cover(functools.partial(fwd_body, phase, True), fdep, width // 4)
+
+    def u_strips(phase):
+        par = phase % 2 if isinstance(phase, int) else lax.rem(phase, 2)
+        return col_copies(ubase.at[par * BANKED], fdep, u_send.at[par], u_recv.at[par])
+
+    def fwd_close(phase):
+        fwd_sweeps(phase)[3]()
+        last = phase * PHASE + (PHASE - 1)
+        for at in (pl.ds(org - PHASE, PHASE), pl.ds(org + width, PHASE)):
+            for b in range(nb):
+                reaction(inner[PHASE - 2, b, at, :], last, b, at)
+
+    def fwd_turn(phase, _):
+        for copy in u_strips(phase):
             copy.wait()
 
         @pl.when(phase == 0)
         def _():
             for copy in fcopies:
                 copy.wait()
-        sides()
-        last = phase * PHASE + (PHASE - 1)
-        for at in (pl.ds(org - PHASE, PHASE), pl.ds(org + width, PHASE)):
-            for b in range(nb):
-                reaction(inner[PHASE - 2, b, at, :], last, b, at)
-
-        @pl.when(phase < phases - 1)
-        def _():
-            for copy in col_copies(ubase.at[(1 - par) * BANKED], fdep, u_send.at[1 - par], u_recv.at[1 - par]):
-                copy.start()
-        return 0
-
-    lax.fori_loop(0, phases, fwd_phase, 0)
-
-    arrive(2, lbase.at[0], None)
-    for copy in col_copies(lbase.at[0], adep, l_send.at[0], l_recv.at[0]):
-        copy.start()
-    depart(ubase.at[phases % 2 * BANKED], 0, uo_ref, 1.0 / scale)
-    acc[...] = jnp.zeros(acc.shape, jnp.float32)
-
-    def adj_phase(phase, _):
-        par = lax.rem(phase, 2)
-
-        def step_body(j, base, cols):
-            src, dst, t = level(lbase, par, j - 1), level(lbase, par, j), steps - (phase * PHASE + j)
-            gain = gains_ref[t]
-            at = pl.ds(base, cols)
-
-            def centre(b, mid):
-                acc[b, at, :] += gain * mid
-                return coef[t, b, at, :]
-            sums = stencil_blocks(lambda b, d: src[b, pl.ds(base + d, cols), :], flip, centre, nb)
-            for b in range(nb):
-                dst[b, at, :] = sums[b]
-
-        first, middle, sides = cover(step_body, adep)
+        early, first, middle, _ = fwd_sweeps(phase + 1)
+        early()
+        fwd_close(phase)
+        for copy in u_strips(phase + 1):
+            copy.start()
         first()
         middle()
-        for copy in col_copies(lbase.at[par * BANKED], adep, l_send.at[par], l_recv.at[par]):
-            copy.wait()
-        sides()
-
-        @pl.when(phase < phases - 1)
-        def _():
-            for copy in col_copies(lbase.at[(1 - par) * BANKED], adep, l_send.at[1 - par], l_recv.at[1 - par]):
-                copy.start()
         return 0
 
-    lax.fori_loop(0, phases, adj_phase, 0)
-
+    fwd_sweeps(0)[2]()
+    lax.fori_loop(0, phases - 1, fwd_turn, 0)
+
+    arrive(2, lbase.at[0], None)
+    for copy in l_strips(0):
+        copy.start()
+    acc[...] = jnp.zeros(acc.shape, jnp.float32)
+    for copy in u_strips(phases - 1):
+        copy.wait()
+    early, first, middle, _ = adj_sweeps(0)
+    early()
+    fwd_close(phases - 1)
+    first()
+    middle()
+    depart(ubase.at[phases % 2 * BANKED], 0, uo_ref, 1.0 / scale)
+    lax.fori_loop(0, phases - 1, adj_turn, 0)
+    for copy in l_strips(phases - 1):
+        copy.wait()
+    adj_sweeps(phases - 1)[3]()
     lo_ref[...] = lbase[phases % 2 * BANKED, :, pl.ds(org, width), :]
 
 

time: 48 us -> 47.8 us (level)
  Pallas kernels: 47.3 us -> 46.8 us
where the time goes in v8:
time: 47.8 us; the launch traced here: 47.7 us
  Pallas kernels  46.8 us (98%)
  between operations  0.82 us (2%)
    pallas_call x1, Pallas kernels, local_run(): pl.pallas_call(functools.partial(kernel, row_size, col_size, core_size, (...  45.7 us
    pallas_call x1, Pallas kernels, local_run(): pl.pallas_call(functools.partial(unlane, (rows, width), 2 * PHASE), out_s...  1.19 us

profile of v8, /device:TPU:97, one launch (start us, length us, event | category | flops | bytes accessed | tf_op | source)
XLA Modules:
  0.0 47.7 jit_solution(3723211928945871169)
XLA Ops:
  0.6 45.7 %steps.1 = (f32[512,256]{1,0:T(8,128)S(1)}, f32[5,256,128]{2,1,0:T(8,128)S(1)}, f32[5,296,128]{2,1,0:T(8,128)S(1)}) custom-call(f32[3,3]{1,0:T(4,128)} %wts_hbm.1, f32[32]{0:T(128)} %gains_hbm.1, f32[512,256]{1,0:T(8,128)} %u_hbm.1, f32[512,256]{1,0:T(8,128)} %f_hbm.1, f32[512,256]{1,0:T(8,128)} %w_hbm.1), custom_call_target="tpu_custom_call" | custom-call | tf_op jit(solution)/shard_map/steps/pallas_call | solution.py:307
  46.3 1.2 %unlane.1 = (f32[512,256]{1,0:T(8,128)}, f32[512,256]{1,0:T(8,128)}, f32[512,256]{1,0:T(8,128)}) custom-call(f32[512,256]{1,0:T(8,128)S(1)} %get-tuple-element.6.u_ref, f32[5,256,128]{2,1,0:T(8,128)S(1)} %get-tuple-element.7.l_ref, f32[5,296,128]{2,1,0:T(8,128)S(1)} %get-tuple-element.8.a_ref), custom_call_target="tpu_custom_call" | custom-call | tf_op jit(solution)/shard_map/unlane/pallas_call | solution.py:336

commit v9 on v8

--- a/solution.py
+++ b/solution.py
@@ -195,14 +195,17 @@
         at = pl.ds(base, cols)
 
         def centre(b, mid):
-            acc[b, at, :] += gain * mid
+            if isinstance(phase, int) and phase == 0 and j == 1:
+                acc[b, at, :] = gain * mid
+            else:
+                acc[b, at, :] += gain * mid
             return coef[t, b, at, :]
         sums = stencil_blocks(lambda b, d: src[b, pl.ds(base + d, cols), :], flip, centre, nb)
         for b in range(nb):
             dst[b, at, :] = sums[b]
 
     def adj_sweeps(phase):
-        return cover(functools.partial(adj_body, phase), adep, width // 2)
+        return cover(functools.partial(adj_body, phase), adep, width * 5 // 8)
 
     def l_strips(phase):
         par = phase % 2 if isinstance(phase, int) else lax.rem(phase, 2)
@@ -257,7 +260,8 @@
     arrive(2, lbase.at[0], None)
     for copy in l_strips(0):
         copy.start()
-    acc[...] = jnp.zeros(acc.shape, jnp.float32)
+    for at in (pl.ds(0, org + 8), pl.ds(org + width - 8, org + 8)):
+        acc[:, at, :] = jnp.zeros((nb, org + 8, LANES), jnp.float32)
     for copy in u_strips(phases - 1):
         copy.wait()
     early, first, middle, _ = adj_sweeps(0)
@@ -265,12 +269,15 @@
     fwd_close(phases - 1)
     first()
     middle()
-    depart(ubase.at[phases % 2 * BANKED], 0, uo_ref, 1.0 / scale)
     lax.fori_loop(0, phases - 1, adj_turn, 0)
+    inside = width - 2 * PHASE
+    lo_ref[:, pl.ds(PHASE, inside), :] = lbase[phases % 2 * BANKED, :, pl.ds(org + PHASE, inside), :]
     for copy in l_strips(phases - 1):
         copy.wait()
+    depart(ubase.at[phases % 2 * BANKED], 0, uo_ref, 1.0 / scale)
     adj_sweeps(phases - 1)[3]()
-    lo_ref[...] = lbase[phases % 2 * BANKED, :, pl.ds(org, width), :]
+    for edge in (0, width - PHASE):
+        lo_ref[:, pl.ds(edge, PHASE), :] = lbase[phases % 2 * BANKED, :, pl.ds(org + edge, PHASE), :]
 
 
 def unlane(tiles, org, u_ref, l_ref, a_ref, uo_hbm, go_hbm, gf_hbm, nat, sem):

time: 47.8 us -> 47.6 us (level)
  no operation moved by 1% of the time
where the time goes in v9:
time: 47.6 us; the launch traced here: 47.5 us
  Pallas kernels  46.7 us (98%)
  between operations  0.82 us (2%)
    pallas_call x1, Pallas kernels, local_run(): pl.pallas_call(functools.partial(kernel, row_size, col_size, core_size, (...  45.5 us
    pallas_call x1, Pallas kernels, local_run(): pl.pallas_call(functools.partial(unlane, (rows, width), 2 * PHASE), out_s...  1.19 us

profile of v9, /device:TPU:97, one launch (start us, length us, event | category | flops | bytes accessed | tf_op | source)
XLA Modules:
  0.0 47.5 jit_solution(324404671331887053)
XLA Ops:
  0.6 45.5 %steps.1 = (f32[512,256]{1,0:T(8,128)S(1)}, f32[5,256,128]{2,1,0:T(8,128)S(1)}, f32[5,296,128]{2,1,0:T(8,128)S(1)}) custom-call(f32[3,3]{1,0:T(4,128)} %wts_hbm.1, f32[32]{0:T(128)} %gains_hbm.1, f32[512,256]{1,0:T(8,128)} %u_hbm.1, f32[512,256]{1,0:T(8,128)} %f_hbm.1, f32[512,256]{1,0:T(8,128)} %w_hbm.1), custom_call_target="tpu_custom_call" | custom-call | tf_op jit(solution)/shard_map/steps/pallas_call | solution.py:314
  46.2 1.2 %unlane.1 = (f32[512,256]{1,0:T(8,128)}, f32[512,256]{1,0:T(8,128)}, f32[512,256]{1,0:T(8,128)}) custom-call(f32[512,256]{1,0:T(8,128)S(1)} %get-tuple-element.6.u_ref, f32[5,256,128]{2,1,0:T(8,128)S(1)} %get-tuple-element.7.l_ref, f32[5,296,128]{2,1,0:T(8,128)S(1)} %get-tuple-element.8.a_ref), custom_call_target="tpu_custom_call" | custom-call | tf_op jit(solution)/shard_map/unlane/pallas_call | solution.py:343

commit v10 on v9

--- a/solution.py
+++ b/solution.py
@@ -164,9 +164,8 @@
         return base.at[(1 - par) * BANKED] if j == PHASE else inner.at[j - 1]
 
     def reaction(val, t, b, at):
-        sq = val * val
-        weight = mid_wt - sq
-        coef[t, b, at, :] = (weight - sq) - sq
+        weight = mid_wt - val * val
+        coef[t, b, at, :] = weight
         return weight
 
     def fwd_body(phase, forced, j, base, cols):
@@ -199,7 +198,7 @@
                 acc[b, at, :] = gain * mid
             else:
                 acc[b, at, :] += gain * mid
-            return coef[t, b, at, :]
+            return 3.0 * coef[t, b, at, :] - 2.0 * mid_wt
         sums = stencil_blocks(lambda b, d: src[b, pl.ds(base + d, cols), :], flip, centre, nb)
         for b in range(nb):
             dst[b, at, :] = sums[b]

time: 47.6 us -> 47.4 us (level)
  no operation moved by 1% of the time
where the time goes in v10:
time: 47.4 us; the launch traced here: 47.3 us
  Pallas kernels  46.4 us (98%)
  between operations  0.82 us (2%)
    pallas_call x1, Pallas kernels, local_run(): pl.pallas_call(functools.partial(kernel, row_size, col_size, core_size, (...  45.3 us
    pallas_call x1, Pallas kernels, local_run(): pl.pallas_call(functools.partial(unlane, (rows, width), 2 * PHASE), out_s...  1.19 us

profile of v10, /device:TPU:97, one launch (start us, length us, event | category | flops | bytes accessed | tf_op | source)
XLA Modules:
  0.0 47.3 jit_solution(17995710735102228854)
XLA Ops:
  0.6 45.3 %steps.1 = (f32[512,256]{1,0:T(8,128)S(1)}, f32[5,256,128]{2,1,0:T(8,128)S(1)}, f32[5,296,128]{2,1,0:T(8,128)S(1)}) custom-call(f32[3,3]{1,0:T(4,128)} %wts_hbm.1, f32[32]{0:T(128)} %gains_hbm.1, f32[512,256]{1,0:T(8,128)} %u_hbm.1, f32[512,256]{1,0:T(8,128)} %f_hbm.1, f32[512,256]{1,0:T(8,128)} %w_hbm.1), custom_call_target="tpu_custom_call" | custom-call | tf_op jit(solution)/shard_map/steps/pallas_call | solution.py:313
  45.9 1.2 %unlane.1 = (f32[512,256]{1,0:T(8,128)}, f32[512,256]{1,0:T(8,128)}, f32[512,256]{1,0:T(8,128)}) custom-call(f32[512,256]{1,0:T(8,128)S(1)} %get-tuple-element.6.u_ref, f32[5,256,128]{2,1,0:T(8,128)S(1)} %get-tuple-element.7.l_ref, f32[5,296,128]{2,1,0:T(8,128)S(1)} %get-tuple-element.8.a_ref), custom_call_target="tpu_custom_call" | custom-call | tf_op jit(solution)/shard_map/unlane/pallas_call | solution.py:342

commit v11 on v10

--- a/solution.py
+++ b/solution.py
@@ -129,7 +129,7 @@
     for copy in col_copies(ubase.at[0], fdep, u_send.at[0], u_recv.at[0]):
         copy.start()
     wts = [[wts_ref[i, j] for j in range(3)] for i in range(3)]
-    flip = [[wts_ref[2 - i, 2 - j] for j in range(3)] for i in range(3)]
+    flip = [[wts_ref[2 - i, 2 - j] * (1.0 / 3.0) for j in range(3)] for i in range(3)]
     mid_wt = wts_ref[1, 1] + DT
 
     def sweep(body, base, count):
@@ -190,7 +190,7 @@
     def adj_body(phase, j, base, cols):
         par = phase % 2 if isinstance(phase, int) else lax.rem(phase, 2)
         src, dst, t = level(lbase, par, j - 1), level(lbase, par, j), steps - (phase * PHASE + j)
-        gain = gains_ref[t]
+        gain = gains_ref[t] * 3.0 ** (j - 1)
         at = pl.ds(base, cols)
 
         def centre(b, mid):
@@ -198,10 +198,10 @@
                 acc[b, at, :] = gain * mid
             else:
                 acc[b, at, :] += gain * mid
-            return 3.0 * coef[t, b, at, :] - 2.0 * mid_wt
+            return coef[t, b, at, :] - mid_wt * (2.0 / 3.0)
         sums = stencil_blocks(lambda b, d: src[b, pl.ds(base + d, cols), :], flip, centre, nb)
         for b in range(nb):
-            dst[b, at, :] = sums[b]
+            dst[b, at, :] = sums[b] * 3.0 ** PHASE if j == PHASE else sums[b]
 
     def adj_sweeps(phase):
         return cover(functools.partial(adj_body, phase), adep, width * 5 // 8)

time: 47.4 us -> 46.9 us (0.989)
  no operation moved by 1% of the time
where the time goes in v11:
time: 46.9 us; the launch traced here: 46.8 us
  Pallas kernels  46 us (98%)
  between operations  0.82 us (2%)
    pallas_call x1, Pallas kernels, local_run(): pl.pallas_call(functools.partial(kernel, row_size, col_size, core_size, (...  44.8 us
    pallas_call x1, Pallas kernels, local_run(): pl.pallas_call(functools.partial(unlane, (rows, width), 2 * PHASE), out_s...  1.19 us

profile of v11, /device:TPU:97, one launch (start us, length us, event | category | flops | bytes accessed | tf_op | source)
XLA Modules:
  0.0 46.8 jit_solution(8875122937542674147)
XLA Ops:
  0.6 44.8 %steps.1 = (f32[512,256]{1,0:T(8,128)S(1)}, f32[5,256,128]{2,1,0:T(8,128)S(1)}, f32[5,296,128]{2,1,0:T(8,128)S(1)}) custom-call(f32[3,3]{1,0:T(4,128)} %wts_hbm.1, f32[32]{0:T(128)} %gains_hbm.1, f32[512,256]{1,0:T(8,128)} %u_hbm.1, f32[512,256]{1,0:T(8,128)} %f_hbm.1, f32[512,256]{1,0:T(8,128)} %w_hbm.1), custom_call_target="tpu_custom_call" | custom-call | tf_op jit(solution)/shard_map/steps/pallas_call | solution.py:313
  45.4 1.2 %unlane.1 = (f32[512,256]{1,0:T(8,128)}, f32[512,256]{1,0:T(8,128)}, f32[512,256]{1,0:T(8,128)}) custom-call(f32[512,256]{1,0:T(8,128)S(1)} %get-tuple-element.6.u_ref, f32[5,256,128]{2,1,0:T(8,128)S(1)} %get-tuple-element.7.l_ref, f32[5,296,128]{2,1,0:T(8,128)S(1)} %get-tuple-element.8.a_ref), custom_call_target="tpu_custom_call" | custom-call | tf_op jit(solution)/shard_map/unlane/pallas_call | solution.py:342

commit v12 on v11

--- a/solution.py
+++ b/solution.py
@@ -204,7 +204,7 @@
             dst[b, at, :] = sums[b] * 3.0 ** PHASE if j == PHASE else sums[b]
 
     def adj_sweeps(phase):
-        return cover(functools.partial(adj_body, phase), adep, width * 5 // 8)
+        return cover(functools.partial(adj_body, phase), adep, width * 11 // 16)
 
     def l_strips(phase):
         par = phase % 2 if isinstance(phase, int) else lax.rem(phase, 2)
@@ -223,7 +223,7 @@
         return 0
 
     def fwd_sweeps(phase):
-        return cover(functools.partial(fwd_body, phase, True), fdep, width // 4)
+        return cover(functools.partial(fwd_body, phase, True), fdep, width * 3 // 8)
 
     def u_strips(phase):
         par = phase % 2 if isinstance(phase, int) else lax.rem(phase, 2)

time: 46.9 us -> 47 us (level)
  no operation moved by 1% of the time
where the time goes in v12:
time: 47 us; the launch traced here: 46.9 us
  Pallas kernels  46.1 us (98%)
  between operations  0.82 us (2%)
    pallas_call x1, Pallas kernels, local_run(): pl.pallas_call(functools.partial(kernel, row_size, col_size, core_size, (...  44.9 us
    pallas_call x1, Pallas kernels, local_run(): pl.pallas_call(functools.partial(unlane, (rows, width), 2 * PHASE), out_s...  1.19 us

profile of v12, /device:TPU:97, one launch (start us, length us, event | category | flops | bytes accessed | tf_op | source)
XLA Modules:
  0.0 46.9 jit_solution(439495159427649157)
XLA Ops:
  0.6 44.9 %steps.1 = (f32[512,256]{1,0:T(8,128)S(1)}, f32[5,256,128]{2,1,0:T(8,128)S(1)}, f32[5,296,128]{2,1,0:T(8,128)S(1)}) custom-call(f32[3,3]{1,0:T(4,128)} %wts_hbm.1, f32[32]{0:T(128)} %gains_hbm.1, f32[512,256]{1,0:T(8,128)} %u_hbm.1, f32[512,256]{1,0:T(8,128)} %f_hbm.1, f32[512,256]{1,0:T(8,128)} %w_hbm.1), custom_call_target="tpu_custom_call" | custom-call | tf_op jit(solution)/shard_map/steps/pallas_call | solution.py:313
  45.5 1.2 %unlane.1 = (f32[512,256]{1,0:T(8,128)}, f32[512,256]{1,0:T(8,128)}, f32[512,256]{1,0:T(8,128)}) custom-call(f32[512,256]{1,0:T(8,128)S(1)} %get-tuple-element.6.u_ref, f32[5,256,128]{2,1,0:T(8,128)S(1)} %get-tuple-element.7.l_ref, f32[5,296,128]{2,1,0:T(8,128)S(1)} %get-tuple-element.8.a_ref), custom_call_target="tpu_custom_call" | custom-call | tf_op jit(solution)/shard_map/unlane/pallas_call | solution.py:342
